TPU v7x, 32 devices: a whole 2x2x4 slice. The times are simulated.
32 devices in a mesh: row: 8 (over z, core), col: 4 (over y, x).
Axes of the slice: x: 2, y: 2, z: 4, core: 2. Of those that a mesh axis runs over, the one named last changes fastest.
Arguments:
- basis: float32 [8192, 1024], P('row', 'col'), may hold values from -6 to 6
- merge_coef: float32 [1024, 4096], P('row', 'col'), may hold values from -0.1875 to 0.1875
- panels: float32 [2, 8192, 256], P(None, ('row', 'col')), may hold values from -0.0625 to 0.0625
- factors: float32 [2, 256, 256], replicated, may hold values from -1 to 1
Outputs:
- vectors: float32 [8192, 4096], P(('row', 'col'))
- wsum: float32 [2, 256], replicated
All inputs are finite; a program needn't handle non-finite values.
Results may differ from a plain program's by a relative error of at most 0.0001.
Values sent between devices are 32-bit elements; how exact they have to be, the bound alone decides.
No kernel may reach another device: no remote copies, remote signals or barrier semaphores. Data moves between devices by JAX's collectives and lax.ppermute only.
A program may use at most 128 MiB of HBM per device.

v0:
```python
import jax
import jax.numpy as jnp
from jax import lax
from jax.sharding import PartitionSpec as P

HI = lax.Precision.HIGHEST


def matmul(left, right):
    return jnp.dot(left, right, precision=HI, preferred_element_type=jnp.float32)


def to_tall(block):
    return lax.all_to_all(block, "col", split_axis=0, concat_axis=1, tiled=True)


def per_device(basis, merge_coef, panels, factors):
    coef = lax.all_gather(merge_coef, "row", axis=0, tiled=True)
    block = matmul(lax.all_gather(basis, "col", axis=1, tiled=True), coef)
    upper = jnp.triu(factors)
    local_v = lax.all_gather(panels, "col", axis=1, tiled=True)

    def reduce_terms(terms):
        return lax.psum(terms, "row")

    field = block
    first = local_v[0]
    second = local_v[1]
    proj_one = reduce_terms(matmul(first.T, field))
    field = field - matmul(first, matmul(upper[0], proj_one))
    proj_two = reduce_terms(matmul(second.T, field))
    field = field - matmul(second, matmul(upper[1], proj_two))
    row_one = jnp.sum(proj_one, axis=1)
    row_two = jnp.sum(proj_two, axis=1)
    row_one, row_two = lax.psum((row_one, row_two), "col")
    field = to_tall(field)
    scale = jnp.sqrt(jnp.float32(field.shape[1]))
    return (field, jnp.stack([row_one, row_two]) / scale)


def solution(mesh):
    placed = (P("row", "col"), P("row", "col"), P(None, ("row", "col"), None), P())
    return jax.shard_map(
        per_device,
        mesh=mesh,
        in_specs=placed,
        out_specs=(P(("row", "col"), None), P()),
        check_vma=False,
    )
```

profile of v0, /device:TPU:0, one launch (start us, length us, event | category | flops | bytes accessed | tf_op | source)
XLA Modules:
  0.0 370.3 jit_solution(15266776425502628769)
XLA Ops:
  7.2 0.0 all-gather.4.cloned.1.call-start
  7.2 0.7 all-gather.4.cloned.1.call-update
  7.9 0.0 all-gather.6.cloned.1.call-start
  7.9 0.7 all-gather.6.cloned.1.call-update
  8.6 0.0 all-gather.8.cloned.1.call-start
  8.7 0.7 all-gather.8.cloned.1.call-update
  9.4 0.0 all-reduce.4.cloned.1.call-start
  9.4 55.6 %all-gather.4.cloned.1.call-done = f32[1024,1024]{1,0:T(8,128)} async-done(((f32[1024,256]{1,0:T(8,128)}), f32[1024,1024]{1,0:T(8,128)}) %all-gather.4.cloned.1.call-update) | async-done | bytes 4194320 | tf_op jit(solution)/shard_map/all_gather | solution.py:19
  65.0 48.5 %all-gather.6.cloned.1.call-done = f32[1024,1024]{1,0:T(8,128)} async-done(((f32[128,1024]{1,0:T(8,128)}), f32[1024,1024]{1,0:T(8,128)}) %all-gather.6.cloned.1.call-update) | async-done | bytes 4194320 | tf_op jit(solution)/shard_map/all_gather | solution.py:18
  113.5 17.5 %fusion.2 = f32[1024,1024]{1,0:T(8,128)} fusion(f32[1024,1024]{1,0:T(8,128)} %all-gather.4.cloned.1.call-done, f32[1024,1024]{1,0:T(8,128)} %all-gather.6.cloned.1.call-done), kind=kOutput, calls=%fused_computation.14 | convolution fusion | flops 12884901888 | bytes 12582912 | tf_op jit(solution)/shard_map/dot_general | solution.py:10
  131.0 0.0 copy-start.4
  131.0 18.4 %all-gather.8.cloned.1.call-done = f32[2,1024,256]{2,1,0:T(8,128)} async-done(((f32[2,256,256]{2,1,0:T(8,128)}), f32[2,1024,256]{2,1,0:T(8,128)}) %all-gather.8.cloned.1.call-update) | async-done | bytes 2097168 | tf_op jit(solution)/shard_map/all_gather | solution.py:21
  149.4 0.0 copy-start.1
  149.4 10.3 %convolution_bitcast_fusion.1 = f32[256,1024]{0,1:T(8,128)} fusion(f32[1024,1024]{1,0:T(8,128)} %fusion.2, f32[2,1024,256]{2,1,0:T(8,128)} %all-gather.8.cloned.1.call-done), kind=kOutput, calls=%fused_computation.3 | convolution fusion | flops 3221225472 | bytes 6291456 | tf_op jit(solution)/shard_map/dot_general | solution.py:10
  159.7 0.0 all-reduce.4.cloned.1.call-update
  159.7 0.0 all-reduce.6.cloned.1.call-start
  159.8 0.1 iota_compare_fusion
  159.9 0.0 copy-done.4
  159.9 0.1 broadcast_select_fusion
  159.9 59.2 %all-reduce.4.cloned.1.call-done = f32[256,1024]{0,1:T(8,128)} async-done(((f32[256,1024]{0,1:T(8,128)}), f32[256,1024]{0,1:T(8,128)}) %all-reduce.4.cloned.1.call-update) | async-done | bytes 1048592 | tf_op jit(solution)/shard_map/psum | solution.py:24
  219.2 2.3 fusion.1
  221.4 0.0 copy-done.1
  221.4 5.7 %bitcast_subtract_fusion.1 = f32[1024,1024]{1,0:T(8,128)S(1)} fusion(f32[1024,1024]{1,0:T(8,128)} %fusion.2, f32[256,1024]{1,0:T(8,128)S(1)} %fusion.1, f32[2,1024,256]{2,1,0:T(8,128)S(1)} %copy-done.1), kind=kOutput, calls=%fused_computation.1 | convolution fusion | flops 3222274048 | bytes 10485760 | tf_op jit(solution)/shard_map/dot_general | solution.py:10
  227.1 0.0 copy-start
  227.1 2.0 copy-done
  229.1 7.8 %convolution_bitcast_fusion = f32[256,1024]{0,1:T(8,128)} fusion(f32[1024,1024]{1,0:T(8,128)S(1)} %bitcast_subtract_fusion.1, f32[2,1024,256]{2,1,0:T(8,128)S(1)} %copy-done.1), kind=kOutput, calls=%fused_computation.2 | convolution fusion | flops 3221225472 | bytes 6291456 | tf_op jit(solution)/shard_map/dot_general | solution.py:10
  237.0 0.0 all-reduce.6.cloned.1.call-update
  237.0 58.5 %all-reduce.6.cloned.1.call-done = f32[256,1024]{0,1:T(8,128)} async-done(((f32[256,1024]{0,1:T(8,128)}), f32[256,1024]{0,1:T(8,128)}) %all-reduce.6.cloned.1.call-update) | async-done | bytes 1048592 | tf_op jit(solution)/shard_map/psum | solution.py:24
  295.5 2.3 fusion
  297.7 6.7 %bitcast_subtract_fusion = f32[1024,1024]{1,0:T(8,128)} fusion(f32[1024,1024]{1,0:T(8,128)} %copy-done, f32[256,1024]{1,0:T(8,128)S(1)} %fusion, f32[2,1024,256]{2,1,0:T(8,128)S(1)} %copy-done.1), kind=kOutput, calls=%fused_computation | convolution fusion | flops 3222274048 | bytes 10485760 | tf_op jit(solution)/shard_map/dot_general | solution.py:10
  304.4 0.0 copy-start.2
  304.4 0.0 copy-start.3
  304.4 5.0 %all-to-all-start = ((f32[4,256,1024]{2,1,0:T(8,128)}), f32[4,256,1024]{2,1,0:T(8,128)}, u32[]{:S(2)}, u32[]{:S(2)}) async-start(f32[4,256,1024]{2,1,0:T(8,128)} %bitcast.36), calls=%async_computation | async-start | bytes 8388608 | tf_op jit(solution)/shard_map/all_to_all | solution.py:14
  309.4 0.0 copy-done.2
  309.4 0.2 reduce_sum.18
  309.6 0.0 copy-done.3
  309.6 0.2 reduce_sum.19
  309.7 48.7 %all-reduce = (f32[1,256]{1,0:T(1,128)S(1)}, f32[1,256]{1,0:T(1,128)S(1)}) all-reduce(f32[1,256]{1,0:T(1,128)S(1)} %bitcast.39, f32[1,256]{1,0:T(1,128)S(1)} %bitcast.38), channel_id=1, replica_groups=mesh['row'=8,'col'=4] {'col'}, use_global_device_ids=true, to_apply=%region_5.6 | all-reduce | flops 512 | bytes 4096 | tf_op jit(solution)/shard_map/psum | solution.py:35
  358.4 0.6 maximum_multiply_fusion
  359.0 0.0 all-to-all-done
  359.0 4.8 %copy.7 = f32[4,32,8,1024]{3,2,0,1:T(8,128)} copy(f32[4,32,8,1024]{3,2,1,0:T(8,128)} %bitcast.12) | data formatting | bytes 8388608 | tf_op jit(solution)/shard_map/all_to_all | solution.py:14
  (1 shorter events, 0.0 us)
Async XLA Ops:
  7.2 57.8 %all-gather.4.cloned.1.call-start = ((), (), s32[]{:S(2)}) async-start(), calls=%async_computation.1 | async-start | bytes 5242880 | tf_op jit(solution)/shard_map/all_gather | solution.py:19
  7.9 105.6 %all-gather.6.cloned.1.call-start = ((), (), s32[]{:S(2)}) async-start(), calls=%async_computation.2 | async-start | bytes 4718592 | tf_op jit(solution)/shard_map/all_gather | solution.py:18
  8.6 140.7 %all-gather.8.cloned.1.call-start = ((), (), s32[]{:S(2)}) async-start(), calls=%async_computation.3 | async-start | bytes 2621440 | tf_op jit(solution)/shard_map/all_gather | solution.py:21
  9.4 209.8 %all-reduce.4.cloned.1.call-start = ((), (), s32[]{:S(2)}) async-start(), calls=%async_computation.4 | async-start | bytes 2097152 | tf_op jit(solution)/shard_map/psum | solution.py:24
  131.0 28.9 %copy-start.4 = (f32[2,256,256]{2,1,0:T(8,128)S(1)}, f32[2,256,256]{2,1,0:T(8,128)}, u32[]{:S(2)}) copy-start(f32[2,256,256]{2,1,0:T(8,128)} %param.7) | copy-start | bytes 1572868
  149.4 72.1 %copy-start.1 = (f32[2,1024,256]{2,1,0:T(8,128)S(1)}, f32[2,1024,256]{2,1,0:T(8,128)}, u32[]{:S(2)}) copy-start(f32[2,1024,256]{2,1,0:T(8,128)} %all-gather.8.cloned.1.call-done) | copy-start | bytes 6291460
  159.7 135.8 %all-reduce.6.cloned.1.call-start = ((), (), s32[]{:S(2)}) async-start(), calls=%async_computation.5 | async-start | bytes 2097152 | tf_op jit(solution)/shard_map/psum | solution.py:24
  227.1 2.0 copy-start
  304.4 5.0 %copy-start.2 = (f32[256,1024]{0,1:T(8,128)S(1)}, f32[256,1024]{0,1:T(8,128)}, u32[]{:S(2)}) copy-start(f32[256,1024]{0,1:T(8,128)} %all-reduce.4.cloned.1.call-done) | copy-start | bytes 3145732
  304.4 5.1 %copy-start.3 = (f32[256,1024]{0,1:T(8,128)S(1)}, f32[256,1024]{0,1:T(8,128)}, u32[]{:S(2)}) copy-start(f32[256,1024]{0,1:T(8,128)} %all-reduce.6.cloned.1.call-done) | copy-start | bytes 3145732
  304.4 54.5 %all-to-all-start = ((f32[4,256,1024]{2,1,0:T(8,128)}), f32[4,256,1024]{2,1,0:T(8,128)}, u32[]{:S(2)}, u32[]{:S(2)}) async-start(f32[4,256,1024]{2,1,0:T(8,128)} %bitcast.36), calls=%async_computation | async-start | bytes 8388608 | tf_op jit(solution)/shard_map/all_to_all | solution.py:14
Sparse Core Ops, SparseCore 0:
  9.8 55.1 all-gather.3
  66.6 46.8 all-gather.5
  115.3 33.9 all-gather.7
  159.8 59.2 all-reduce.3
  237.1 58.2 all-reduce.5
where the time goes:
time: 371 us; the launch traced here: 370 us
  waiting for transfers between devices  242 us (65%)
  matrix products  52.5 us (14%)
  blocking collectives  48.7 us (13%)
  between operations  13.9 us (4%)
  local copies, waits for them, and re-layouts  6.81 us (2%)
  starting transfers between devices  5.16 us (1%)
    psum x2, waiting for transfers between devices, reduce_terms(): return lax.psum(terms, 'row')  118 us
    all_gather x1, waiting for transfers between devices, per_device(): block = matmul(lax.all_gather(basis, 'col', axis=1, tiled=True), coef)  55.6 us
    dot_general x7, matrix products, matmul(): jnp.dot(left, right, precision=HI, preferred_element_type=jnp.float32)  52.5 us
    psum x1, blocking collectives, per_device(): row_one, row_two = lax.psum((row_one, row_two), 'col')  48.7 us
    all_gather x1, waiting for transfers between devices, per_device(): coef = lax.all_gather(merge_coef, 'row', axis=0, tiled=True)  48.5 us
    all_gather x1, waiting for transfers between devices, per_device(): local_v = lax.all_gather(panels, 'col', axis=1, tiled=True)  18.4 us
  transfers between devices with their start and end apart: 6, of which 5 were waited for; matrix products, arithmetic and copies ran while one was open for 5% of the time, Pallas kernels for 0%

commit v1 on v0

v1 whole, which is shorter than its diff:
```python
import jax
import jax.numpy as jnp
from jax import lax
from jax.experimental import pallas as pl
from jax.experimental.pallas import tpu as pltpu
from jax.sharding import PartitionSpec as P


BOTH = ("row", "col")


F32 = jnp.float32
ROWS_ROWS = (((0,), (0,)), ((), ()))
COLS_COLS = (((1,), (1,)), ((), ()))
PLAIN = (((1,), (0,)), ((), ()))


def masks(bits, core):
    order = list(range(bits)) if core == 0 else list(range(bits))[::-1]
    out = [0]
    for b in order:
        out = out + [m ^ (1 << b) for m in out]
    return out


def split3(x):
    hi = x.astype(jnp.bfloat16)
    return hi, (x - hi.astype(F32)).astype(jnp.bfloat16)


def mul(left, right, dims=PLAIN):
    def one(a, b):
        return lax.dot_general(a, b, dims, preferred_element_type=F32)

    return one(left[0], right[0]) + (one(left[0], right[1]) + one(left[1], right[0]))


def pick(core, pair):
    return jnp.where(core == 0, pair[0], pair[1])


class Plan:
    def __init__(self, mesh):
        self.n_row, self.n_col = mesh.shape["row"], mesh.shape["col"]
        self.n_z = self.n_row // 2
        self.col_bits, self.z_bits = self.n_col.bit_length() - 1, self.n_z.bit_length() - 1
        self.col_masks = [masks(self.col_bits, core) for core in range(2)]
        self.z_masks = [masks(self.z_bits, core) for core in range(2)]
        self.col_twin = [self.col_masks[1].index(m) for m in self.col_masks[0]]
        self.groups = [[0]] + [list(range(2**b, 2 ** (b + 1))) for b in range(self.z_bits)]

    def place(self):
        row, col = lax.axis_index("row"), lax.axis_index("col")
        return row // 2, lax.rem(row, 2), col

    def col_of(self, col, core, slot):
        return col ^ pick(core, [m[slot] for m in self.col_masks])

    def z_of(self, z, core, slot):
        return z ^ pick(core, [m[slot] for m in self.z_masks])

    def permute(self, x, to):
        pairs = [(r * self.n_col + c, to(r, c)) for r in range(self.n_row) for c in range(self.n_col)]
        return lax.ppermute(x, BOTH, pairs)

    def over_col(self, x, slot):
        return self.permute(x, lambda r, c: r * self.n_col + (c ^ self.col_masks[r % 2][slot]))

    def over_z(self, x, slot):
        return self.permute(x, lambda r, c: (r ^ (2 * self.z_masks[r % 2][slot])) * self.n_col + c)

    def over_core(self, x):
        return self.permute(x, lambda r, c: (r ^ 1) * self.n_col + c)


def project(plan, basis, vecs, sums):
    n_col, kb = plan.n_col, basis.shape[1]
    part, nb = vecs[0].shape[1:]
    half = kb // 2
    blk = sums.shape[1]
    cuts = nb // kb
    height = (2 + cuts) * nb + 8

    def body(basis_ref, sums_ref, *refs):
        v, (keep, send, total) = refs[:n_col], refs[n_col:]
        z, core, col = plan.place()
        proj, cross = [0.0, 0.0], 0.0
        for s in range(n_col):
            at = pl.multiple_of(plan.col_of(col, core, s) * part, part)
            b = split3(basis_ref[pl.ds(at, part), :])
            v0, v1 = split3(v[s][0]), split3(v[s][1])
            proj[0] += mul(v0, b, ROWS_ROWS)
            proj[1] += mul(v1, b, ROWS_ROWS)
            cross += mul(v1, v0, ROWS_ROWS)
        total[:nb, :] = proj[0]
        total[nb : 2 * nb, :] = proj[1]
        for i in range(cuts):
            total[(2 + i) * nb : (3 + i) * nb, :] = cross[:, i * kb : (i + 1) * kb]
        per = kb // blk if kb >= blk else 1
        line = lax.broadcasted_iota(jnp.int32, (8, kb), 0) * per + lax.broadcasted_iota(jnp.int32, (8, kb), 1) // blk
        wide = jnp.concatenate([sums_ref[:1, :]] * per, axis=1)
        total[height - 8 :, :] = jnp.where(line == z * 2 + core, jnp.broadcast_to(wide, (8, kb)), 0.0)
        left, right = total[:, :half], total[:, half:]
        keep[...] = jnp.where(core == 0, left, right)
        send[...] = jnp.where(core == 0, right, left)

    out = jax.ShapeDtypeStruct((height, half), F32)
    return pl.pallas_call(
        body,
        out_shape=(out, out),
        scratch_shapes=[pltpu.VMEM((height, kb), F32)],
        compiler_params=pltpu.CompilerParams(vmem_limit_bytes=16 * 2**20),
        cost_estimate=pl.CostEstimate(flops=36 * part * n_col * nb * kb, bytes_accessed=4 * (3 * part * n_col * kb + height * kb), transcendentals=0),
        name="project",
    )(basis, sums, *vecs)


def update(plan, basis, vecs, factors, mine, theirs):
    n_col, kb = plan.n_col, basis.shape[1]
    part, nb = vecs[0].shape[1:]
    height, _ = mine.shape
    cuts = nb // kb
    tail = 8

    def body(basis_ref, factors_ref, mine_ref, theirs_ref, *refs):
        v, outs = refs[:n_col], refs[n_col:]
        _, core, col = plan.place()
        left = jnp.where(core == 0, mine_ref[...], theirs_ref[...])
        right = jnp.where(core == 0, theirs_ref[...], mine_ref[...])
        total = jnp.concatenate([left, right], axis=1)
        keep = lax.broadcasted_iota(jnp.int32, (nb, nb), 0) <= lax.broadcasted_iota(jnp.int32, (nb, nb), 1)
        upper = [split3(jnp.where(keep, factors_ref[i], 0.0)) for i in range(2)]
        one, two = total[:nb], total[nb : 2 * nb]
        cross = jnp.concatenate([total[(2 + i) * nb : (3 + i) * nb] for i in range(cuts)], axis=1)
        first = mul(upper[0], split3(one))
        split_first = split3(first)
        two = two - mul(split3(cross), split_first)
        split_second = split3(mul(upper[1], split3(two)))
        line = lax.broadcasted_iota(jnp.int32, (8, kb), 0)
        weight = jnp.sum(jnp.where(line == col, total[height - 8 :], 0.0), axis=0, keepdims=True)
        weight = split3(jnp.broadcast_to(weight, (8, kb)))
        shares = [mul(weight, split3(g), COLS_COLS)[:1] for g in (one, two)]
        shares = [x[:, i * kb : (i + 1) * kb] for x in shares for i in range(cuts)]
        shares = jnp.concatenate(shares + [jnp.zeros((tail - 2 * cuts, kb), F32)], axis=0)
        for s in range(n_col):
            at = pl.multiple_of(plan.col_of(col, core, s) * part, part)
            b = basis_ref[pl.ds(at, part), :]
            b = b - mul(split3(v[s][0]), split_first) - mul(split3(v[s][1]), split_second)
            outs[s][:part, :] = b
            outs[s][part:, :] = shares

    out = jax.ShapeDtypeStruct((part + tail, kb), F32)
    return pl.pallas_call(
        body,
        out_shape=(out,) * n_col,
        compiler_params=pltpu.CompilerParams(vmem_limit_bytes=16 * 2**20),
        cost_estimate=pl.CostEstimate(flops=12 * part * n_col * nb * kb, bytes_accessed=4 * (4 * part * n_col * kb + height * kb), transcendentals=0),
        name="update",
    )(basis, factors, mine, theirs, *vecs)


def product(plan, b2, pieces, others):
    n_col, groups = plan.n_col, plan.groups
    kb = b2[0].shape[1]
    rows = b2[0].shape[0] - 8
    blk, width = pieces[0][0].shape
    depth = kb * n_col
    tile = 256
    flat = [x for g in pieces for x in g] + [x for g in others for x in g]
    half = len(groups) * n_col

    def body(*refs):
        b, c = refs[:n_col], refs[n_col : n_col + 2 * half]
        out, cbuf, obuf, bhi, blo, in_sem, out_sem = refs[n_col + 2 * half :]
        z, core, col = plan.place()

        def fetch(s, slot):
            copies = []
            for side in range(2):
                who = core if side == 0 else 1 - core
                t = s if side == 0 else plan.col_twin[s]
                for g, zslots in enumerate(groups):
                    for i, zslot in enumerate(zslots):
                        at = pl.multiple_of((plan.z_of(z, who, zslot) * 2 + who) * blk, blk)
                        copies.append(
                            pltpu.make_async_copy(
                                c[side * half + g * n_col + t].at[pl.ds(i * blk, blk), :],
                                cbuf.at[slot, pl.ds(at, blk), :],
                                in_sem.at[slot, len(copies)],
                            )
                        )
            return copies

        def store(s, slot):
            at = pl.multiple_of(plan.col_of(col, core, s) * width, width)
            return pltpu.make_async_copy(obuf.at[slot], out.at[:, pl.ds(at, width)], out_sem.at[slot])

        for cp in fetch(0, 0):
            cp.start()
        for s in range(n_col):
            hi, lo = split3(b[s][:rows, :])
            at = pl.multiple_of(plan.col_of(col, core, s) * kb, kb)
            bhi[:, pl.ds(at, kb)] = hi
            blo[:, pl.ds(at, kb)] = lo
        for s in range(n_col):
            slot = s % 2
            if s + 1 < n_col:
                for cp in fetch(s + 1, 1 - slot):
                    cp.start()
            for cp in fetch(s, slot):
                cp.wait()
            if s >= 2:
                store(s - 2, slot).wait()

            @pl.loop(0, width // tile)
            def _(t, slot=slot):
                cols = pl.ds(pl.multiple_of(t * tile, tile), tile)
                obuf[slot, :, cols] = mul((bhi[...], blo[...]), split3(cbuf[slot, :, cols]))

            store(s, slot).start()
        for s in range(max(0, n_col - 2), n_col):
            store(s, s % 2).wait()

    anywhere = pl.BlockSpec(memory_space=pl.ANY)
    return pl.pallas_call(
        body,
        out_shape=jax.ShapeDtypeStruct((rows, width * n_col), F32),
        in_specs=[pl.BlockSpec(memory_space=pltpu.VMEM)] * n_col + [anywhere] * len(flat),
        out_specs=anywhere,
        scratch_shapes=[
            pltpu.VMEM((2, depth, width), F32),
            pltpu.VMEM((2, rows, width), F32),
            pltpu.VMEM((rows, depth), jnp.bfloat16),
            pltpu.VMEM((rows, depth), jnp.bfloat16),
            pltpu.SemaphoreType.DMA((2, 2 * plan.n_z)),
            pltpu.SemaphoreType.DMA((2,)),
        ],
        compiler_params=pltpu.CompilerParams(vmem_limit_bytes=24 * 2**20),
        cost_estimate=pl.CostEstimate(flops=6 * rows * depth * width * n_col, bytes_accessed=4 * (depth + rows) * width * n_col, transcendentals=0),
        name="product",
    )(*b2, *flat)


def spread(plan, x):
    found = [x]
    for step in range(plan.col_bits):
        found = found + [plan.over_col(y, 2**step) for y in found]
    return found


def solution(mesh):
    plan = Plan(mesh)

    def per_device(basis, coef, panels, factors):
        nb, kb = panels.shape[2], basis.shape[1]
        part = panels.shape[1]
        n_col, z_bits = plan.n_col, plan.z_bits
        _, core, _ = plan.place()

        vecs = spread(plan, panels)
        sums = jnp.broadcast_to(jnp.sum(coef, axis=1)[None, :], (8, coef.shape[0]))
        for step in range(plan.col_bits):
            sums = sums + plan.over_col(sums, 2**step)

        parts, held = [coef], coef
        for step in range(z_bits):
            got = plan.over_z(held, 2**step)
            parts.append(got)
            if step + 1 < z_bits:
                held = jnp.concatenate([held, got], axis=0)
        pieces = [spread(plan, x) for x in parts]
        others = [[plan.over_core(x) for x in found] for found in pieces]

        keep, send = project(plan, basis, vecs, sums)
        mine = keep + plan.over_core(send)
        for step in range(z_bits):
            mine = mine + plan.over_z(mine, 2**step)
        theirs = plan.over_core(mine)
        sends = update(plan, basis, vecs, factors, mine, theirs)

        tall = [sends[0]] + [plan.over_col(sends[s], s) for s in range(1, n_col)]
        shares = [x[part : part + 2 * nb // kb].reshape(2, nb) for x in tall]
        by_mask = [pick(core, [shares[m.index(i)] for m in plan.col_masks]) for i in range(n_col)]
        while len(by_mask) > 1:
            by_mask = [by_mask[i] + by_mask[i + 1] for i in range(0, len(by_mask), 2)]
        wsum = by_mask[0] / jnp.sqrt(F32(coef.shape[1] * n_col))
        return product(plan, tall, pieces, others), wsum

    placed = (P("row", "col"), P("row", "col"), P(None, ("row", "col"), None), P())
    return jax.shard_map(
        per_device,
        mesh=mesh,
        in_specs=placed,
        out_specs=(P(("row", "col"), None), P()),
        check_vma=False,
    )
```

time: 371 us -> 153 us (0.41)
  waiting for transfers between devices: 242 us -> 81.5 us
  matrix products: 52.5 us -> 0 us
  blocking collectives: 48.7 us -> 0 us
  starting transfers between devices: 5.16 us -> 29.8 us
  Pallas kernels: 0 us -> 16 us
  between operations: 13.9 us -> 0.85 us
  local copies, waits for them, and re-layouts: 6.81 us -> 19.6 us
    all_gather x3 -> x0, waiting for transfers between devices: 122 us -> none  [the longest x1 55.6 us: per_device(): block = matmul(lax.all_gather(basis, 'col', axis=1, tiled=True), coef)]
    psum x2 -> x0, waiting for transfers between devices: 118 us -> none  [reduce_terms(): return lax.psum(terms, 'row')]
    ppermute x0 -> x35, waiting for transfers between devices: none -> 81.5 us  [permute(): return lax.ppermute(x, BOTH, pairs)]
    dot_general x7 -> x0, matrix products: 52.5 us -> none  [matmul(): jnp.dot(left, right, precision=HI, preferred_element_type=jnp.float32)]
    psum x1 -> x0, blocking collectives: 48.7 us -> none  [per_device(): row_one, row_two = lax.psum((row_one, row_two), 'col')]
    ppermute x0 -> x35, starting transfers between devices: none -> 29.8 us  [permute(): return lax.ppermute(x, BOTH, pairs)]
    unnamed x10 -> x58, local copies, waits for them, and re-layouts: 2.02 us -> 19.6 us
    pallas_call x0 -> x3, Pallas kernels: none -> 16 us  [the longest x1 12.6 us: product(): pl.pallas_call(body, out_shape=jax.ShapeDtypeStruct((rows, width * n_col)...]
  transfers between devices with their start and end apart: 6 -> 35, of which waited for: 5 -> 15; matrix products, arithmetic and copies ran while one was open for 5% -> 3% of each run, Pallas kernels for 0% -> 2%
where the time goes in v1:
time: 153 us; the launch traced here: 152 us
  waiting for transfers between devices  81.5 us (53%)
  starting transfers between devices  29.8 us (19%)
  local copies, waits for them, and re-layouts  19.6 us (13%)
  Pallas kernels  16 us (10%)
  other arithmetic  3.98 us (3%)
    ppermute x35, waiting for transfers between devices, permute(): return lax.ppermute(x, BOTH, pairs)  81.5 us
    ppermute x35, starting transfers between devices, permute(): return lax.ppermute(x, BOTH, pairs)  29.8 us
    unnamed x58, local copies, waits for them, and re-layouts  19.6 us
    pallas_call x1, Pallas kernels, product(): pl.pallas_call(body, out_shape=jax.ShapeDtypeStruct((rows, width * n_col)...  12.6 us
  transfers between devices with their start and end apart: 35, of which 15 were waited for; matrix products, arithmetic and copies ran while one was open for 3% of the time, Pallas kernels for 2%

profile of v1, /device:TPU:0, one launch (start us, length us, event | category | flops | bytes accessed | tf_op | source)
XLA Modules:
  0.0 151.7 jit_solution(16074925766441337300)
XLA Ops:
  0.6 3.1 %collective-permute-start.15 = (f32[128,1024]{1,0:T(8,128)}, f32[128,1024]{1,0:T(8,128)S(1)}, u32[]{:S(2)}, u32[]{:S(2)}) collective-permute-start(f32[128,1024]{1,0:T(8,128)} %refs_4_.1), channel_id=1, source_target_pairs={{0,8},{1,9},{2,10},{3,11},{4,20},{5,21},{6,22},{7,23},{8,0},{9,1},... | collective-permute-start | bytes 1572872 | tf_op jit(solution)/shard_map/ppermute | solution.py:64
  3.7 1.5 collective-permute-start.2
  5.2 11.2 %collective-permute-done.15.refs_8_ = f32[128,1024]{1,0:T(8,128)S(1)} collective-permute-done((f32[128,1024]{1,0:T(8,128)}, f32[128,1024]{1,0:T(8,128)S(1)}, u32[]{:S(2)}, u32[]{:S(2)}) %collective-permute-start.15) | collective-permute-done | bytes 524320 | tf_op jit(solution)/shard_map/ppermute | solution.py:64
  16.4 2.1 %pad_maximum_fusion = f32[256,1024]{1,0:T(8,128)} fusion(f32[128,1024]{1,0:T(8,128)S(1)} %collective-permute-done.15.refs_8_, f32[128,1024]{1,0:T(8,128)} %refs_4_.1), kind=kLoop, calls=%fused_computation | loop fusion | flops 262144 | bytes 2097152 | tf_op jit(solution)/shard_map/concatenate | solution.py:270
  18.5 2.4 %collective-permute-start.19 = (f32[256,1024]{1,0:T(8,128)}, f32[256,1024]{1,0:T(8,128)}, u32[]{:S(2)}, u32[]{:S(2)}) collective-permute-start(f32[256,1024]{1,0:T(8,128)} %pad_maximum_fusion), channel_id=1, source_target_pairs={{0,16},{1,17},{2,18},{3,19},{4,12},{5,13},{6,14},{7,15},{8,24},{9,... | collective-permute-start | bytes 3145736 | tf_op jit(solution)/shard_map/ppermute | solution.py:64
  20.9 1.5 %collective-permute-start.3 = (f32[2,256,256]{2,1,0:T(8,128)}, f32[2,256,256]{2,1,0:T(8,128)S(1)}, u32[]{:S(2)}, u32[]{:S(2)}) collective-permute-start(f32[2,256,256]{2,1,0:T(8,128)} %refs_0_.3), channel_id=1, source_target_pairs={{0,2},{1,3},{2,0},{3,1},{4,5},{5,4},{6,7},{7,6},{8,10},{9,11},{10,... | collective-permute-start | bytes 1572872 | tf_op jit(solution)/shard_map/ppermute | solution.py:64
  22.4 0.5 collective-permute-start.4
  22.9 1.2 reduce_sum.9
  24.1 1.6 %collective-permute-start = (f32[8,128]{1,0:T(8,128)S(1)}, f32[8,128]{1,0:T(8,128)S(1)}, u32[]{:S(2)}, u32[]{:S(2)}) collective-permute-start(f32[8,128]{1,0:T(8,128)S(1)} %broadcast_in_dim.2), channel_id=1, source_target_pairs={{0,1},{1,0},{2,3},{3,2},{4,6},{5,7},{6,4},{7,5},{8,9},{9,8},{10,11... | collective-permute-start | bytes 12296 | tf_op jit(solution)/shard_map/ppermute | solution.py:64
  25.6 2.2 %collective-permute-done = f32[8,128]{1,0:T(8,128)S(1)} collective-permute-done((f32[8,128]{1,0:T(8,128)S(1)}, f32[8,128]{1,0:T(8,128)S(1)}, u32[]{:S(2)}, u32[]{:S(2)}) %collective-permute-start) | collective-permute-done | bytes 4128 | tf_op jit(solution)/shard_map/ppermute | solution.py:64
  27.8 1.5 %collective-permute-start.1 = (f32[8,128]{1,0:T(8,128)S(1)}, f32[8,128]{1,0:T(8,128)S(1)}, u32[]{:S(2)}, u32[]{:S(2)}) collective-permute-start(f32[8,128]{1,0:T(8,128)S(1)} %broadcast_add_fusion), channel_id=1, source_target_pairs={{0,2},{1,3},{2,0},{3,1},{4,5},{5,4},{6,7},{7,6},{8,10},{9,11},{10,... | collective-permute-start | bytes 12296 | tf_op jit(solution)/shard_map/ppermute | solution.py:64
  29.3 1.5 collective-permute-start.12
  30.8 10.8 %collective-permute-done.1 = f32[8,128]{1,0:T(8,128)S(1)} collective-permute-done((f32[8,128]{1,0:T(8,128)S(1)}, f32[8,128]{1,0:T(8,128)S(1)}, u32[]{:S(2)}, u32[]{:S(2)}) %collective-permute-start.1) | collective-permute-done | bytes 4128 | tf_op jit(solution)/shard_map/ppermute | solution.py:64
  41.6 1.5 %collective-permute-start.13 = (f32[128,1024]{1,0:T(8,128)}, f32[128,1024]{1,0:T(8,128)S(1)}, u32[]{:S(2)}, u32[]{:S(2)}) collective-permute-start(f32[128,1024]{1,0:T(8,128)} %refs_4_.1), channel_id=1, source_target_pairs={{0,2},{1,3},{2,0},{3,1},{4,5},{5,4},{6,7},{7,6},{8,10},{9,11},{10,... | collective-permute-start | bytes 1572872 | tf_op jit(solution)/shard_map/ppermute | solution.py:64
  43.1 1.2 copy-done.1
  44.4 1.0 copy-done.3
  45.4 1.4 project.1
  46.9 0.6 collective-permute-start.5
  47.4 1.5 collective-permute-start.16
  48.9 0.5 collective-permute-start.20
  49.4 0.5 collective-permute-start.17
  50.0 2.0 %collective-permute-done.13.refs_6_ = f32[128,1024]{1,0:T(8,128)S(1)} collective-permute-done((f32[128,1024]{1,0:T(8,128)}, f32[128,1024]{1,0:T(8,128)S(1)}, u32[]{:S(2)}, u32[]{:S(2)}) %collective-permute-start.13) | collective-permute-done | bytes 524320 | tf_op jit(solution)/shard_map/ppermute | solution.py:64
  52.0 2.4 %collective-permute-start.6 = (f32[776,128]{1,0:T(8,128)S(1)}, f32[776,128]{1,0:T(8,128)S(1)}, u32[]{:S(2)}, u32[]{:S(2)}) collective-permute-start(f32[776,128]{1,0:T(8,128)S(1)} %add.26), channel_id=1, source_target_pairs={{0,8},{1,9},{2,10},{3,11},{4,20},{5,21},{6,22},{7,23},{8,0},{9,1},... | collective-permute-start | bytes 1191944 | tf_op jit(solution)/shard_map/ppermute | solution.py:64
  54.4 7.0 %collective-permute-done.16.refs_9_ = f32[128,1024]{1,0:T(8,128)S(1)} collective-permute-done((f32[128,1024]{1,0:T(8,128)S(1)}, f32[128,1024]{1,0:T(8,128)S(1)}, u32[]{:S(2)}, u32[]{:S(2)}) %collective-permute-start.16) | collective-permute-done | bytes 524320 | tf_op jit(solution)/shard_map/ppermute | solution.py:64
  61.5 0.5 collective-permute-start.14
  62.0 0.6 collective-permute-done.6
  62.6 1.6 %collective-permute-done.17.refs_10_ = f32[128,1024]{1,0:T(8,128)S(1)} collective-permute-done((f32[128,1024]{1,0:T(8,128)S(1)}, f32[128,1024]{1,0:T(8,128)S(1)}, u32[]{:S(2)}, u32[]{:S(2)}) %collective-permute-start.17) | collective-permute-done | bytes 524320 | tf_op jit(solution)/shard_map/ppermute | solution.py:64
  64.2 0.7 collective-permute-start.7
  65.0 0.8 copy-done.13
  66.1 10.1 %collective-permute-done.14.refs_7_ = f32[128,1024]{1,0:T(8,128)S(1)} collective-permute-done((f32[128,1024]{1,0:T(8,128)S(1)}, f32[128,1024]{1,0:T(8,128)S(1)}, u32[]{:S(2)}, u32[]{:S(2)}) %collective-permute-start.14) | collective-permute-done | bytes 524320 | tf_op jit(solution)/shard_map/ppermute | solution.py:64
  76.3 0.6 collective-permute-start.18
  77.3 1.0 collective-permute-start.21
  78.3 2.9 %collective-permute-done.20.refs_13_ = f32[256,1024]{1,0:T(8,128)} collective-permute-done((f32[256,1024]{1,0:T(8,128)}, f32[256,1024]{1,0:T(8,128)}, u32[]{:S(2)}, u32[]{:S(2)}) %collective-permute-start.20) | collective-permute-done | bytes 1048608 | tf_op jit(solution)/shard_map/ppermute | solution.py:64
  81.3 0.8 copy-done.17
  82.1 0.5 collective-permute-start.28
  82.6 2.9 %collective-permute-done.18.refs_11_ = f32[128,1024]{1,0:T(8,128)} collective-permute-done((f32[128,1024]{1,0:T(8,128)S(1)}, f32[128,1024]{1,0:T(8,128)}, u32[]{:S(2)}, u32[]{:S(2)}) %collective-permute-start.18) | collective-permute-done | bytes 524320 | tf_op jit(solution)/shard_map/ppermute | solution.py:64
  85.5 0.5 collective-permute-start.26
  86.1 1.9 %update.1 = (f32[264,256]{1,0:T(8,128)S(1)}, f32[264,256]{1,0:T(8,128)S(1)}, f32[264,256]{1,0:T(8,128)S(1)}, f32[264,256]{1,0:T(8,128)S(1)}) custom-call(f32[1024,256]{1,0:T(8,128)S(1)} %copy-done.1, f32[2,256,256]{2,1,0:T(8,128)S(1)} %copy-done.2, f32[776,128]{1,0:T(8,128)S(1)} %add.28.mine_ref, f32[776,128]{1,0:T(8,128)S(1)} %collective-permute-done.8.theirs_ref, ...), custom_call_target="tpu_custom_call" | custom-call | flops 805306368 | bytes 4988928 | tf_op jit(solution)/shard_map/update/pallas_call | solution.py:153
  88.0 0.8 copy-done.21
  88.8 0.8 collective-permute-start.10
  89.6 0.8 copy-done.23
  90.4 2.2 %collective-permute-start.11 = (f32[264,256]{1,0:T(8,128)S(1)}, f32[264,256]{1,0:T(8,128)S(1)}, u32[]{:S(2)}, u32[]{:S(2)}) collective-permute-start(f32[264,256]{1,0:T(8,128)S(1)} %get-tuple-element.13), channel_id=1, source_target_pairs={{0,3},{1,2},{2,1},{3,0},{4,7},{5,6},{6,5},{7,4},{8,11},{9,10},{10,... | collective-permute-start | bytes 811016 | tf_op jit(solution)/shard_map/ppermute | solution.py:64
  92.6 0.8 copy-done.25
  93.4 5.2 %collective-permute-done.21.refs_14_ = f32[256,1024]{1,0:T(8,128)} collective-permute-done((f32[256,1024]{1,0:T(8,128)}, f32[256,1024]{1,0:T(8,128)}, u32[]{:S(2)}, u32[]{:S(2)}) %collective-permute-start.21) | collective-permute-done | bytes 1048608 | tf_op jit(solution)/shard_map/ppermute | solution.py:64
  98.6 18.0 %collective-permute-done.10.refs_2_ = f32[264,256]{1,0:T(8,128)S(1)} collective-permute-done((f32[264,256]{1,0:T(8,128)S(1)}, f32[264,256]{1,0:T(8,128)S(1)}, u32[]{:S(2)}, u32[]{:S(2)}) %collective-permute-start.10) | collective-permute-done | bytes 270368 | tf_op jit(solution)/shard_map/ppermute | solution.py:64
  116.6 0.5 collective-permute-start.34
  117.1 1.5 collective-permute-start.9
  118.6 5.0 %collective-permute-done.9.refs_1_ = f32[264,256]{1,0:T(8,128)S(1)} collective-permute-done((f32[264,256]{1,0:T(8,128)S(1)}, f32[264,256]{1,0:T(8,128)S(1)}, u32[]{:S(2)}, u32[]{:S(2)}) %collective-permute-start.9) | collective-permute-done | bytes 270368 | tf_op jit(solution)/shard_map/ppermute | solution.py:64
  123.6 0.6 fusion.1
  124.2 1.5 collective-permute-done.30.refs_23_
  125.7 0.8 copy-done.27
  126.6 1.0 copy-done.6
  127.6 1.0 copy-done.8
  128.6 1.0 copy-done.10
  129.7 1.0 copy-done.12
  130.7 1.0 copy-done.14
  131.8 1.0 copy-done.16
  132.8 1.0 copy-done.18
  133.8 1.0 copy-done.20
  134.9 1.0 copy-done.22
  135.9 1.0 copy-done.24
  137.0 1.0 copy-done.26
  138.0 1.0 copy-done.28
  139.1 12.6 %product.1 = f32[256,4096]{1,0:T(8,128)} custom-call(f32[264,256]{1,0:T(8,128)S(1)} %get-tuple-element.10.refs_0_, f32[264,256]{1,0:T(8,128)S(1)} %collective-permute-done.9.refs_1_, f32[264,256]{1,0:T(8,128)S(1)} %collective-permute-done.10.refs_2_, f32[264,256]{1,0:T(8,128)S(1)} %collective-permute-done.11.refs_3_, f32[128,1024]{1,0:T(8,128)S(1)} %copy-done, ...), custom_call_target="tpu_custom_call" | custom-call | flops 6442450944 | bytes 20971520 | tf_op jit(solution)/shard_map/product/pallas_call | solution.py:225
  (76 shorter events, 1.1 us)
Async XLA Ops:
  0.6 15.8 %collective-permute-start.15 = (f32[128,1024]{1,0:T(8,128)}, f32[128,1024]{1,0:T(8,128)S(1)}, u32[]{:S(2)}, u32[]{:S(2)}) collective-permute-start(f32[128,1024]{1,0:T(8,128)} %refs_4_.1), channel_id=1, source_target_pairs={{0,8},{1,9},{2,10},{3,11},{4,20},{5,21},{6,22},{7,23},{8,0},{9,1},... | collective-permute-start | bytes 1572872 | tf_op jit(solution)/shard_map/ppermute | solution.py:64
  3.7 18.6 %collective-permute-start.2 = (f32[2,256,256]{2,1,0:T(8,128)}, f32[2,256,256]{2,1,0:T(8,128)S(1)}, u32[]{:S(2)}, u32[]{:S(2)}) collective-permute-start(f32[2,256,256]{2,1,0:T(8,128)} %refs_0_.3), channel_id=1, source_target_pairs={{0,1},{1,0},{2,3},{3,2},{4,6},{5,7},{6,4},{7,5},{8,9},{9,8},{10,11... | collective-permute-start | bytes 1572872 | tf_op jit(solution)/shard_map/ppermute | solution.py:64
  18.5 30.4 %collective-permute-start.19 = (f32[256,1024]{1,0:T(8,128)}, f32[256,1024]{1,0:T(8,128)}, u32[]{:S(2)}, u32[]{:S(2)}) collective-permute-start(f32[256,1024]{1,0:T(8,128)} %pad_maximum_fusion), channel_id=1, source_target_pairs={{0,16},{1,17},{2,18},{3,19},{4,12},{5,13},{6,14},{7,15},{8,24},{9,... | collective-permute-start | bytes 3145736 | tf_op jit(solution)/shard_map/ppermute | solution.py:64
  20.9 22.2 %collective-permute-start.3 = (f32[2,256,256]{2,1,0:T(8,128)}, f32[2,256,256]{2,1,0:T(8,128)S(1)}, u32[]{:S(2)}, u32[]{:S(2)}) collective-permute-start(f32[2,256,256]{2,1,0:T(8,128)} %refs_0_.3), channel_id=1, source_target_pairs={{0,2},{1,3},{2,0},{3,1},{4,5},{5,4},{6,7},{7,6},{8,10},{9,11},{10,... | collective-permute-start | bytes 1572872 | tf_op jit(solution)/shard_map/ppermute | solution.py:64
  22.4 20.7 %collective-permute-start.4 = (f32[2,256,256]{2,1,0:T(8,128)S(1)}, f32[2,256,256]{2,1,0:T(8,128)S(1)}, u32[]{:S(2)}, u32[]{:S(2)}) collective-permute-start(f32[2,256,256]{2,1,0:T(8,128)S(1)} %collective-permute-done.2.refs_1_), channel_id=1, source_target_pairs={{0,2},{1,3},{2,0},{3,1},{4,5},{5,4},{6,7},{7,6},{8,10},{9,11},{10,... | collective-permute-start | bytes 1572872 | tf_op jit(solution)/shard_map/ppermute | solution.py:64
  24.1 3.7 %collective-permute-start = (f32[8,128]{1,0:T(8,128)S(1)}, f32[8,128]{1,0:T(8,128)S(1)}, u32[]{:S(2)}, u32[]{:S(2)}) collective-permute-start(f32[8,128]{1,0:T(8,128)S(1)} %broadcast_in_dim.2), channel_id=1, source_target_pairs={{0,1},{1,0},{2,3},{3,2},{4,6},{5,7},{6,4},{7,5},{8,9},{9,8},{10,11... | collective-permute-start | bytes 12296 | tf_op jit(solution)/shard_map/ppermute | solution.py:64
  27.8 13.8 %collective-permute-start.1 = (f32[8,128]{1,0:T(8,128)S(1)}, f32[8,128]{1,0:T(8,128)S(1)}, u32[]{:S(2)}, u32[]{:S(2)}) collective-permute-start(f32[8,128]{1,0:T(8,128)S(1)} %broadcast_add_fusion), channel_id=1, source_target_pairs={{0,2},{1,3},{2,0},{3,1},{4,5},{5,4},{6,7},{7,6},{8,10},{9,11},{10,... | collective-permute-start | bytes 12296 | tf_op jit(solution)/shard_map/ppermute | solution.py:64
  29.3 18.1 %collective-permute-start.12 = (f32[128,1024]{1,0:T(8,128)}, f32[128,1024]{1,0:T(8,128)S(1)}, u32[]{:S(2)}, u32[]{:S(2)}) collective-permute-start(f32[128,1024]{1,0:T(8,128)} %refs_4_.1), channel_id=1, source_target_pairs={{0,1},{1,0},{2,3},{3,2},{4,6},{5,7},{6,4},{7,5},{8,9},{9,8},{10,11... | collective-permute-start | bytes 1572872 | tf_op jit(solution)/shard_map/ppermute | solution.py:64
  41.6 10.4 %collective-permute-start.13 = (f32[128,1024]{1,0:T(8,128)}, f32[128,1024]{1,0:T(8,128)S(1)}, u32[]{:S(2)}, u32[]{:S(2)}) collective-permute-start(f32[128,1024]{1,0:T(8,128)} %refs_4_.1), channel_id=1, source_target_pairs={{0,2},{1,3},{2,0},{3,1},{4,5},{5,4},{6,7},{7,6},{8,10},{9,11},{10,... | collective-permute-start | bytes 1572872 | tf_op jit(solution)/shard_map/ppermute | solution.py:64
  43.1 11.3 %collective-permute-start.23 = (f32[128,1024]{1,0:T(8,128)}, f32[128,1024]{1,0:T(8,128)S(1)}, u32[]{:S(2)}, u32[]{:S(2)}) collective-permute-start(f32[128,1024]{1,0:T(8,128)} %refs_4_.1), channel_id=1, source_target_pairs={{0,4},{1,5},{2,6},{3,7},{4,0},{5,1},{6,2},{7,3},{8,12},{9,13},{10,... | collective-permute-start | bytes 1572872 | tf_op jit(solution)/shard_map/ppermute | solution.py:64
  43.1 1.2 copy-start.1
  44.4 1.0 copy-start.3
  45.4 40.7 %copy-start.2 = (f32[2,256,256]{2,1,0:T(8,128)S(1)}, f32[2,256,256]{2,1,0:T(8,128)}, u32[]{:S(2)}) copy-start(f32[2,256,256]{2,1,0:T(8,128)} %factors_ref.1) | copy-start | bytes 1572868
  45.4 40.7 %copy-start.4 = (f32[2,256,256]{2,1,0:T(8,128)S(1)}, f32[2,256,256]{2,1,0:T(8,128)}, u32[]{:S(2)}) copy-start(f32[2,256,256]{2,1,0:T(8,128)} %refs_0_.3) | copy-start | bytes 1572868
  46.8 79.7 %copy-start = (f32[128,1024]{1,0:T(8,128)S(1)}, f32[128,1024]{1,0:T(8,128)}, u32[]{:S(2)}) copy-start(f32[128,1024]{1,0:T(8,128)} %refs_4_.1) | copy-start | bytes 1572868
  46.9 2.6 %collective-permute-start.5 = (f32[776,128]{1,0:T(8,128)S(1)}, f32[776,128]{1,0:T(8,128)S(1)}, u32[]{:S(2)}, u32[]{:S(2)}) collective-permute-start(f32[776,128]{1,0:T(8,128)S(1)} %get-tuple-element.9), channel_id=1, source_target_pairs={{0,4},{1,5},{2,6},{3,7},{4,0},{5,1},{6,2},{7,3},{8,12},{9,13},{10,... | collective-permute-start | bytes 1191944 | tf_op jit(solution)/shard_map/ppermute | solution.py:64
  47.4 14.0 %collective-permute-start.16 = (f32[128,1024]{1,0:T(8,128)S(1)}, f32[128,1024]{1,0:T(8,128)S(1)}, u32[]{:S(2)}, u32[]{:S(2)}) collective-permute-start(f32[128,1024]{1,0:T(8,128)S(1)} %collective-permute-done.15.refs_8_), channel_id=1, source_target_pairs={{0,1},{1,0},{2,3},{3,2},{4,6},{5,7},{6,4},{7,5},{8,9},{9,8},{10,11... | collective-permute-start | bytes 1572872 | tf_op jit(solution)/shard_map/ppermute | solution.py:64
  48.9 32.3 %collective-permute-start.20 = (f32[256,1024]{1,0:T(8,128)}, f32[256,1024]{1,0:T(8,128)}, u32[]{:S(2)}, u32[]{:S(2)}) collective-permute-start(f32[256,1024]{1,0:T(8,128)} %collective-permute-done.19.refs_12_), channel_id=1, source_target_pairs={{0,1},{1,0},{2,3},{3,2},{4,6},{5,7},{6,4},{7,5},{8,9},{9,8},{10,11... | collective-permute-start | bytes 3145736 | tf_op jit(solution)/shard_map/ppermute | solution.py:64
  49.4 14.8 %collective-permute-start.17 = (f32[128,1024]{1,0:T(8,128)S(1)}, f32[128,1024]{1,0:T(8,128)S(1)}, u32[]{:S(2)}, u32[]{:S(2)}) collective-permute-start(f32[128,1024]{1,0:T(8,128)S(1)} %collective-permute-done.15.refs_8_), channel_id=1, source_target_pairs={{0,2},{1,3},{2,0},{3,1},{4,5},{5,4},{6,7},{7,6},{8,10},{9,11},{10,... | collective-permute-start | bytes 1572872 | tf_op jit(solution)/shard_map/ppermute | solution.py:64
  52.0 71.6 %copy-start.5 = (f32[128,1024]{1,0:T(8,128)}, f32[128,1024]{1,0:T(8,128)S(1)}, u32[]{:S(2)}) copy-start(f32[128,1024]{1,0:T(8,128)S(1)} %collective-permute-done.13.refs_6_) | copy-start | bytes 1572868
  52.0 10.5 %collective-permute-start.6 = (f32[776,128]{1,0:T(8,128)S(1)}, f32[776,128]{1,0:T(8,128)S(1)}, u32[]{:S(2)}, u32[]{:S(2)}) collective-permute-start(f32[776,128]{1,0:T(8,128)S(1)} %add.26), channel_id=1, source_target_pairs={{0,8},{1,9},{2,10},{3,11},{4,20},{5,21},{6,22},{7,23},{8,0},{9,1},... | collective-permute-start | bytes 1191944 | tf_op jit(solution)/shard_map/ppermute | solution.py:64
  54.4 69.2 %copy-start.7 = (f32[128,1024]{1,0:T(8,128)}, f32[128,1024]{1,0:T(8,128)S(1)}, u32[]{:S(2)}) copy-start(f32[128,1024]{1,0:T(8,128)S(1)} %collective-permute-done.23.refs_16_) | copy-start | bytes 1572868
  54.4 10.5 %collective-permute-start.27 = (f32[128,1024]{1,0:T(8,128)S(1)}, f32[128,1024]{1,0:T(8,128)S(1)}, u32[]{:S(2)}, u32[]{:S(2)}) collective-permute-start(f32[128,1024]{1,0:T(8,128)S(1)} %collective-permute-done.15.refs_8_), channel_id=1, source_target_pairs={{0,4},{1,5},{2,6},{3,7},{4,0},{5,1},{6,2},{7,3},{8,12},{9,13},{10,... | collective-permute-start | bytes 1572872 | tf_op jit(solution)/shard_map/ppermute | solution.py:64
  61.5 62.1 %copy-start.9 = (f32[128,1024]{1,0:T(8,128)}, f32[128,1024]{1,0:T(8,128)S(1)}, u32[]{:S(2)}) copy-start(f32[128,1024]{1,0:T(8,128)S(1)} %collective-permute-done.16.refs_9_) | copy-start | bytes 1572868
  61.5 14.8 %collective-permute-start.14 = (f32[128,1024]{1,0:T(8,128)S(1)}, f32[128,1024]{1,0:T(8,128)S(1)}, u32[]{:S(2)}, u32[]{:S(2)}) collective-permute-start(f32[128,1024]{1,0:T(8,128)S(1)} %collective-permute-done.12.refs_5_), channel_id=1, source_target_pairs={{0,2},{1,3},{2,0},{3,1},{4,5},{5,4},{6,7},{7,6},{8,10},{9,11},{10,... | collective-permute-start | bytes 1572872 | tf_op jit(solution)/shard_map/ppermute | solution.py:64
  62.6 18.7 %collective-permute-start.24 = (f32[128,1024]{1,0:T(8,128)S(1)}, f32[128,1024]{1,0:T(8,128)S(1)}, u32[]{:S(2)}, u32[]{:S(2)}) collective-permute-start(f32[128,1024]{1,0:T(8,128)S(1)} %collective-permute-done.12.refs_5_), channel_id=1, source_target_pairs={{0,4},{1,5},{2,6},{3,7},{4,0},{5,1},{6,2},{7,3},{8,12},{9,13},{10,... | collective-permute-start | bytes 1572872 | tf_op jit(solution)/shard_map/ppermute | solution.py:64
  64.2 59.4 %copy-start.11 = (f32[128,1024]{1,0:T(8,128)}, f32[128,1024]{1,0:T(8,128)S(1)}, u32[]{:S(2)}) copy-start(f32[128,1024]{1,0:T(8,128)S(1)} %collective-permute-done.17.refs_10_) | copy-start | bytes 1572868
  64.2 13.0 %collective-permute-start.7 = (f32[776,128]{1,0:T(8,128)S(1)}, f32[776,128]{1,0:T(8,128)S(1)}, u32[]{:S(2)}, u32[]{:S(2)}) collective-permute-start(f32[776,128]{1,0:T(8,128)S(1)} %add.27), channel_id=1, source_target_pairs={{0,16},{1,17},{2,18},{3,19},{4,12},{5,13},{6,14},{7,15},{8,24},{9,... | collective-permute-start | bytes 1191944 | tf_op jit(solution)/shard_map/ppermute | solution.py:64
  65.0 0.8 copy-start.13
  65.8 16.3 %collective-permute-start.25 = (f32[128,1024]{1,0:T(8,128)S(1)}, f32[128,1024]{1,0:T(8,128)S(1)}, u32[]{:S(2)}, u32[]{:S(2)}) collective-permute-start(f32[128,1024]{1,0:T(8,128)S(1)} %collective-permute-done.13.refs_6_), channel_id=1, source_target_pairs={{0,4},{1,5},{2,6},{3,7},{4,0},{5,1},{6,2},{7,3},{8,12},{9,13},{10,... | collective-permute-start | bytes 1572872 | tf_op jit(solution)/shard_map/ppermute | solution.py:64
  76.3 47.4 %copy-start.15 = (f32[128,1024]{1,0:T(8,128)}, f32[128,1024]{1,0:T(8,128)S(1)}, u32[]{:S(2)}) copy-start(f32[128,1024]{1,0:T(8,128)S(1)} %collective-permute-done.14.refs_7_) | copy-start | bytes 1572868
  76.3 9.3 %collective-permute-start.18 = (f32[128,1024]{1,0:T(8,128)S(1)}, f32[128,1024]{1,0:T(8,128)}, u32[]{:S(2)}, u32[]{:S(2)}) collective-permute-start(f32[128,1024]{1,0:T(8,128)S(1)} %collective-permute-done.16.refs_9_), channel_id=1, source_target_pairs={{0,2},{1,3},{2,0},{3,1},{4,5},{5,4},{6,7},{7,6},{8,10},{9,11},{10,... | collective-permute-start | bytes 1572872 | tf_op jit(solution)/shard_map/ppermute | solution.py:64
  77.3 21.3 %collective-permute-start.21 = (f32[256,1024]{1,0:T(8,128)}, f32[256,1024]{1,0:T(8,128)}, u32[]{:S(2)}, u32[]{:S(2)}) collective-permute-start(f32[256,1024]{1,0:T(8,128)} %collective-permute-done.19.refs_12_), channel_id=1, source_target_pairs={{0,2},{1,3},{2,0},{3,1},{4,5},{5,4},{6,7},{7,6},{8,10},{9,11},{10,... | collective-permute-start | bytes 3145736 | tf_op jit(solution)/shard_map/ppermute | solution.py:64
  81.2 35.4 %collective-permute-start.22 = (f32[256,1024]{1,0:T(8,128)}, f32[256,1024]{1,0:T(8,128)}, u32[]{:S(2)}, u32[]{:S(2)}) collective-permute-start(f32[256,1024]{1,0:T(8,128)} %collective-permute-done.20.refs_13_), channel_id=1, source_target_pairs={{0,2},{1,3},{2,0},{3,1},{4,5},{5,4},{6,7},{7,6},{8,10},{9,11},{10,... | collective-permute-start | bytes 3145736 | tf_op jit(solution)/shard_map/ppermute | solution.py:64
  81.3 0.8 copy-start.17
  82.1 3.4 %collective-permute-start.8 = (f32[776,128]{1,0:T(8,128)S(1)}, f32[776,128]{1,0:T(8,128)S(1)}, u32[]{:S(2)}, u32[]{:S(2)}) collective-permute-start(f32[776,128]{1,0:T(8,128)S(1)} %add.28.mine_ref), channel_id=1, source_target_pairs={{0,4},{1,5},{2,6},{3,7},{4,0},{5,1},{6,2},{7,3},{8,12},{9,13},{10,... | collective-permute-start | bytes 1191944 | tf_op jit(solution)/shard_map/ppermute | solution.py:64
  82.1 41.5 %copy-start.19 = (f32[128,1024]{1,0:T(8,128)}, f32[128,1024]{1,0:T(8,128)S(1)}, u32[]{:S(2)}) copy-start(f32[128,1024]{1,0:T(8,128)S(1)} %collective-permute-done.25.refs_18_) | copy-start | bytes 1572868
  82.1 5.9 %collective-permute-start.28 = (f32[128,1024]{1,0:T(8,128)S(1)}, f32[128,1024]{1,0:T(8,128)S(1)}, u32[]{:S(2)}, u32[]{:S(2)}) collective-permute-start(f32[128,1024]{1,0:T(8,128)S(1)} %collective-permute-done.16.refs_9_), channel_id=1, source_target_pairs={{0,4},{1,5},{2,6},{3,7},{4,0},{5,1},{6,2},{7,3},{8,12},{9,13},{10,... | collective-permute-start | bytes 1572872 | tf_op jit(solution)/shard_map/ppermute | solution.py:64
  85.5 4.0 %collective-permute-start.29 = (f32[128,1024]{1,0:T(8,128)S(1)}, f32[128,1024]{1,0:T(8,128)S(1)}, u32[]{:S(2)}, u32[]{:S(2)}) collective-permute-start(f32[128,1024]{1,0:T(8,128)S(1)} %collective-permute-done.17.refs_10_), channel_id=1, source_target_pairs={{0,4},{1,5},{2,6},{3,7},{4,0},{5,1},{6,2},{7,3},{8,12},{9,13},{10,... | collective-permute-start | bytes 1572872 | tf_op jit(solution)/shard_map/ppermute | solution.py:64
  85.5 7.0 %collective-permute-start.26 = (f32[128,1024]{1,0:T(8,128)S(1)}, f32[128,1024]{1,0:T(8,128)S(1)}, u32[]{:S(2)}, u32[]{:S(2)}) collective-permute-start(f32[128,1024]{1,0:T(8,128)S(1)} %collective-permute-done.14.refs_7_), channel_id=1, source_target_pairs={{0,4},{1,5},{2,6},{3,7},{4,0},{5,1},{6,2},{7,3},{8,12},{9,13},{10,... | collective-permute-start | bytes 1572872 | tf_op jit(solution)/shard_map/ppermute | solution.py:64
  88.0 0.8 copy-start.21
  88.8 27.8 %collective-permute-start.10 = (f32[264,256]{1,0:T(8,128)S(1)}, f32[264,256]{1,0:T(8,128)S(1)}, u32[]{:S(2)}, u32[]{:S(2)}) collective-permute-start(f32[264,256]{1,0:T(8,128)S(1)} %get-tuple-element.12), channel_id=1, source_target_pairs={{0,2},{1,3},{2,0},{3,1},{4,5},{5,4},{6,7},{7,6},{8,10},{9,11},{10,... | collective-permute-start | bytes 811016 | tf_op jit(solution)/shard_map/ppermute | solution.py:64
  89.6 0.8 copy-start.23
  90.4 26.7 %collective-permute-start.11 = (f32[264,256]{1,0:T(8,128)S(1)}, f32[264,256]{1,0:T(8,128)S(1)}, u32[]{:S(2)}, u32[]{:S(2)}) collective-permute-start(f32[264,256]{1,0:T(8,128)S(1)} %get-tuple-element.13), channel_id=1, source_target_pairs={{0,3},{1,2},{2,1},{3,0},{4,7},{5,6},{6,5},{7,4},{8,11},{9,10},{10,... | collective-permute-start | bytes 811016 | tf_op jit(solution)/shard_map/ppermute | solution.py:64
  92.6 0.8 copy-start.25
  93.4 33.2 %collective-permute-start.31 = (f32[256,1024]{1,0:T(8,128)}, f32[256,1024]{1,0:T(8,128)}, u32[]{:S(2)}, u32[]{:S(2)}) collective-permute-start(f32[256,1024]{1,0:T(8,128)} %collective-permute-done.19.refs_12_), channel_id=1, source_target_pairs={{0,4},{1,5},{2,6},{3,7},{4,0},{5,1},{6,2},{7,3},{8,12},{9,13},{10,... | collective-permute-start | bytes 3145736 | tf_op jit(solution)/shard_map/ppermute | solution.py:64
  98.6 27.9 %collective-permute-start.32 = (f32[256,1024]{1,0:T(8,128)}, f32[256,1024]{1,0:T(8,128)}, u32[]{:S(2)}, u32[]{:S(2)}) collective-permute-start(f32[256,1024]{1,0:T(8,128)} %collective-permute-done.20.refs_13_), channel_id=1, source_target_pairs={{0,4},{1,5},{2,6},{3,7},{4,0},{5,1},{6,2},{7,3},{8,12},{9,13},{10,... | collective-permute-start | bytes 3145736 | tf_op jit(solution)/shard_map/ppermute | solution.py:64
  116.6 9.9 %collective-permute-start.33 = (f32[256,1024]{1,0:T(8,128)}, f32[256,1024]{1,0:T(8,128)}, u32[]{:S(2)}, u32[]{:S(2)}) collective-permute-start(f32[256,1024]{1,0:T(8,128)} %collective-permute-done.21.refs_14_), channel_id=1, source_target_pairs={{0,4},{1,5},{2,6},{3,7},{4,0},{5,1},{6,2},{7,3},{8,12},{9,13},{10,... | collective-permute-start | bytes 3145736 | tf_op jit(solution)/shard_map/ppermute | solution.py:64
  116.6 9.9 %collective-permute-start.34 = (f32[256,1024]{1,0:T(8,128)}, f32[256,1024]{1,0:T(8,128)}, u32[]{:S(2)}, u32[]{:S(2)}) collective-permute-start(f32[256,1024]{1,0:T(8,128)} %collective-permute-done.22.refs_15_), channel_id=1, source_target_pairs={{0,4},{1,5},{2,6},{3,7},{4,0},{5,1},{6,2},{7,3},{8,12},{9,13},{10,... | collective-permute-start | bytes 3145736 | tf_op jit(solution)/shard_map/ppermute | solution.py:64
  117.1 6.5 %collective-permute-start.9 = (f32[264,256]{1,0:T(8,128)S(1)}, f32[264,256]{1,0:T(8,128)S(1)}, u32[]{:S(2)}, u32[]{:S(2)}) collective-permute-start(f32[264,256]{1,0:T(8,128)S(1)} %get-tuple-element.11), channel_id=1, source_target_pairs={{0,1},{1,0},{2,3},{3,2},{4,6},{5,7},{6,4},{7,5},{8,9},{9,8},{10,11... | collective-permute-start | bytes 811016 | tf_op jit(solution)/shard_map/ppermute | solution.py:64
  123.6 2.1 %collective-permute-start.30 = (f32[128,1024]{1,0:T(8,128)}, f32[128,1024]{1,0:T(8,128)S(1)}, u32[]{:S(2)}, u32[]{:S(2)}) collective-permute-start(f32[128,1024]{1,0:T(8,128)} %collective-permute-done.18.refs_11_), channel_id=1, source_target_pairs={{0,4},{1,5},{2,6},{3,7},{4,0},{5,1},{6,2},{7,3},{8,12},{9,13},{10,... | collective-permute-start | bytes 1572872 | tf_op jit(solution)/shard_map/ppermute | solution.py:64
  125.7 0.8 copy-start.27
  126.5 1.0 copy-start.6
  127.6 1.0 copy-start.8
  128.6 1.0 copy-start.10
  129.7 1.0 copy-start.12
  130.7 1.0 copy-start.14
  131.8 1.0 copy-start.16
  132.8 1.0 copy-start.18
  133.8 1.0 copy-start.20
  134.9 1.0 copy-start.22
  135.9 1.0 copy-start.24
  137.0 1.0 copy-start.26
  138.0 1.0 copy-start.28

commit v2 on v1

--- a/solution.py
+++ b/solution.py
@@ -47,7 +47,9 @@
         self.col_masks = [masks(self.col_bits, core) for core in range(2)]
         self.z_masks = [masks(self.z_bits, core) for core in range(2)]
         self.col_twin = [self.col_masks[1].index(m) for m in self.col_masks[0]]
-        self.groups = [[0]] + [list(range(2**b, 2 ** (b + 1))) for b in range(self.z_bits)]
+
+    def relayed(self, slot):
+        return self.n_z > 2 and self.n_col > 2 and slot == self.n_z // 2
 
     def place(self):
         row, col = lax.axis_index("row"), lax.axis_index("col")
@@ -159,52 +161,57 @@
     )(basis, factors, mine, theirs, *vecs)
 
 
-def product(plan, b2, pieces, others):
-    n_col, groups = plan.n_col, plan.groups
-    kb = b2[0].shape[1]
-    rows = b2[0].shape[0] - 8
+def product(plan, b2, pieces, others, slots, base=None):
+    n_col, n_z = plan.n_col, plan.n_z
     blk, width = pieces[0][0].shape
-    depth = kb * n_col
-    tile = 256
-    flat = [x for g in pieces for x in g] + [x for g in others for x in g]
-    half = len(groups) * n_col
+    depth = blk * plan.n_row
+    kb = depth // n_col
+    rows = b2[0].shape[0] - 8 if base is None else base[0].shape[0]
+    tile = 1024
+    flat = [pieces[g][s] for s in slots for g in range(n_z)] + [others[g][plan.col_twin[s]] for s in slots for g in range(n_z)]
+    half = n_z * len(slots)
+    given = list(b2) if base is None else list(base[1:])
+    more = [] if base is None else [base[0]]
+    n_given = len(given)
 
     def body(*refs):
-        b, c = refs[:n_col], refs[n_col : n_col + 2 * half]
-        out, cbuf, obuf, bhi, blo, in_sem, out_sem = refs[n_col + 2 * half :]
+        b, c = refs[:n_given], refs[n_given : n_given + 2 * half]
+        rest = refs[n_given + 2 * half + len(more) :]
+        if base is None:
+            out, both, cbuf, obuf, in_sem, out_sem = rest
+        else:
+            (both,), (out, cbuf, obuf, in_sem, out_sem) = b, rest
         z, core, col = plan.place()
 
         def fetch(s, slot):
             copies = []
             for side in range(2):
                 who = core if side == 0 else 1 - core
-                t = s if side == 0 else plan.col_twin[s]
-                for g, zslots in enumerate(groups):
-                    for i, zslot in enumerate(zslots):
-                        at = pl.multiple_of((plan.z_of(z, who, zslot) * 2 + who) * blk, blk)
-                        copies.append(
-                            pltpu.make_async_copy(
-                                c[side * half + g * n_col + t].at[pl.ds(i * blk, blk), :],
-                                cbuf.at[slot, pl.ds(at, blk), :],
-                                in_sem.at[slot, len(copies)],
-                            )
+                for g in range(n_z):
+                    at = pl.multiple_of((plan.z_of(z, who, g) * 2 + who) * blk, blk)
+                    copies.append(
+                        pltpu.make_async_copy(
+                            c[side * half + s * n_z + g],
+                            cbuf.at[slot, pl.ds(at, blk), :],
+                            in_sem.at[slot, len(copies)],
                         )
+                    )
             return copies
 
         def store(s, slot):
-            at = pl.multiple_of(plan.col_of(col, core, s) * width, width)
+            at = pl.multiple_of(plan.col_of(col, core, slots[s]) * width, width)
             return pltpu.make_async_copy(obuf.at[slot], out.at[:, pl.ds(at, width)], out_sem.at[slot])
 
         for cp in fetch(0, 0):
             cp.start()
-        for s in range(n_col):
+        for s in range(n_col if base is None else 0):
             hi, lo = split3(b[s][:rows, :])
             at = pl.multiple_of(plan.col_of(col, core, s) * kb, kb)
-            bhi[:, pl.ds(at, kb)] = hi
-            blo[:, pl.ds(at, kb)] = lo
-        for s in range(n_col):
+            both[:rows, pl.ds(at, kb)] = hi
+            both[rows:, pl.ds(at, kb)] = lo
+        for s in range(len(slots)):
             slot = s % 2
-            if s + 1 < n_col:
+            if s + 1 < len(slots):
                 for cp in fetch(s + 1, 1 - slot):
                     cp.start()
             for cp in fetch(s, slot):
@@ -215,30 +222,32 @@
             @pl.loop(0, width // tile)
             def _(t, slot=slot):
                 cols = pl.ds(pl.multiple_of(t * tile, tile), tile)
-                obuf[slot, :, cols] = mul((bhi[...], blo[...]), split3(cbuf[slot, :, cols]))
+                hi, lo = split3(cbuf[slot, :, cols])
+                high = jnp.dot(both[...], hi, preferred_element_type=F32)
+                low = jnp.dot(both[:rows, :], lo, preferred_element_type=F32)
+                obuf[slot, :, cols] = high[:rows] + (high[rows:] + low)
 
             store(s, slot).start()
-        for s in range(max(0, n_col - 2), n_col):
+        for s in range(max(0, len(slots) - 2), len(slots)):
             store(s, s % 2).wait()
 
-    anywhere = pl.BlockSpec(memory_space=pl.ANY)
+    anywhere, near = pl.BlockSpec(memory_space=pl.ANY), pl.BlockSpec(memory_space=pltpu.VMEM)
+    split, n_split = jax.ShapeDtypeStruct((2 * rows, depth), jnp.bfloat16), 1 if base is None else 0
     return pl.pallas_call(
         body,
-        out_shape=jax.ShapeDtypeStruct((rows, width * n_col), F32),
-        in_specs=[pl.BlockSpec(memory_space=pltpu.VMEM)] * n_col + [anywhere] * len(flat),
-        out_specs=anywhere,
+        out_shape=[jax.ShapeDtypeStruct((rows, width * n_col), F32)] + [split] * n_split,
+        in_specs=[near] * n_given + [anywhere] * len(flat + more),
+        out_specs=[anywhere] + [near] * n_split,
         scratch_shapes=[
             pltpu.VMEM((2, depth, width), F32),
             pltpu.VMEM((2, rows, width), F32),
-            pltpu.VMEM((rows, depth), jnp.bfloat16),
-            pltpu.VMEM((rows, depth), jnp.bfloat16),
             pltpu.SemaphoreType.DMA((2, 2 * plan.n_z)),
             pltpu.SemaphoreType.DMA((2,)),
         ],
         compiler_params=pltpu.CompilerParams(vmem_limit_bytes=24 * 2**20),
-        cost_estimate=pl.CostEstimate(flops=6 * rows * depth * width * n_col, bytes_accessed=4 * (depth + rows) * width * n_col, transcendentals=0),
-        name="product",
-    )(*b2, *flat)
+        cost_estimate=pl.CostEstimate(flops=6 * rows * depth * width * len(slots), bytes_accessed=4 * (depth + rows) * width * len(slots), transcendentals=0),
+        input_output_aliases={n_given + 2 * half: 0} if more else {},
+    )(*given, *flat, *more)
 
 
 def spread(plan, x):
@@ -262,13 +271,14 @@
         for step in range(plan.col_bits):
             sums = sums + plan.over_col(sums, 2**step)
 
-        parts, held = [coef], coef
+        parts = [coef]
         for step in range(z_bits):
-            got = plan.over_z(held, 2**step)
-            parts.append(got)
-            if step + 1 < z_bits:
-                held = jnp.concatenate([held, got], axis=0)
-        pieces = [spread(plan, x) for x in parts]
+            parts += [plan.over_z(x, 2**step) for x in parts]
+        pieces = [None if plan.relayed(g) else spread(plan, x) for g, x in enumerate(parts)]
+        for g, x in enumerate(parts):
+            if plan.relayed(g):
+                pieces[g] = [x] + [plan.over_z(pieces[0][t], g) for t in range(1, n_col)]
+                pieces[g][n_col // 2] = plan.over_col(x, n_col // 2)
         others = [[plan.over_core(x) for x in found] for found in pieces]
 
         keep, send = project(plan, basis, vecs, sums)
@@ -284,7 +294,10 @@
         while len(by_mask) > 1:
             by_mask = [by_mask[i] + by_mask[i + 1] for i in range(0, len(by_mask), 2)]
         wsum = by_mask[0] / jnp.sqrt(F32(coef.shape[1] * n_col))
-        return product(plan, tall, pieces, others), wsum
+        first = list(range(n_col - 1))
+        held = product(plan, tall, pieces, others, first)
+        (vectors,) = product(plan, (), pieces, others, [n_col - 1], held)
+        return vectors, wsum
 
     placed = (P("row", "col"), P("row", "col"), P(None, ("row", "col"), None), P())
     return jax.shard_map(

time: 153 us -> 149 us (0.974)
  waiting for transfers between devices: 81.5 us -> 65 us
  starting transfers between devices: 29.8 us -> 38.4 us
  local copies, waits for them, and re-layouts: 19.6 us -> 25 us
    ppermute x35 -> x43, waiting for transfers between devices: 81.5 us -> 65 us  [permute(): return lax.ppermute(x, BOTH, pairs)]
    ppermute x35 -> x43, starting transfers between devices: 29.8 us -> 38.4 us  [permute(): return lax.ppermute(x, BOTH, pairs)]
    unnamed x58 -> x90, local copies, waits for them, and re-layouts: 19.6 us -> 25 us
    concatenate x1 -> x0, other arithmetic: 2.09 us -> none  [per_device(): held = jnp.concatenate([held, got], axis=0)]
    pallas_call x1 -> x2, Pallas kernels: 12.6 us -> 11.8 us  [product(): pl.pallas_call(body, out_shape=[jax.ShapeDtypeStruct((rows, width * n_col...]
  transfers between devices with their start and end apart: 35 -> 43, of which waited for: 15 -> 17; matrix products, arithmetic and copies ran while one was open for 3% -> 2% of each run, Pallas kernels for 2% -> 9%
where the time goes in v2:
time: 149 us; the launch traced here: 148 us
  waiting for transfers between devices  65 us (44%)
  starting transfers between devices  38.4 us (26%)
  local copies, waits for them, and re-layouts  25 us (17%)
  Pallas kernels  15.9 us (11%)
  other arithmetic  2.61 us (2%)
    ppermute x43, waiting for transfers between devices, permute(): return lax.ppermute(x, BOTH, pairs)  65 us
    ppermute x43, starting transfers between devices, permute(): return lax.ppermute(x, BOTH, pairs)  38.4 us
    unnamed x90, local copies, waits for them, and re-layouts  25 us
    pallas_call x2, Pallas kernels, product(): pl.pallas_call(body, out_shape=[jax.ShapeDtypeStruct((rows, width * n_col...  11.8 us
  transfers between devices with their start and end apart: 43, of which 17 were waited for; matrix products, arithmetic and copies ran while one was open for 2% of the time, Pallas kernels for 9%

profile of v2, /device:TPU:0, one launch (start us, length us, event | category | flops | bytes accessed | tf_op | source)
XLA Modules:
  0.0 148.1 jit_solution(4027070968233566274)
XLA Ops:
  0.6 3.0 %collective-permute-start.2 = (f32[2,256,256]{2,1,0:T(8,128)}, f32[2,256,256]{2,1,0:T(8,128)S(1)}, u32[]{:S(2)}, u32[]{:S(2)}) collective-permute-start(f32[2,256,256]{2,1,0:T(8,128)} %refs_0_.3), channel_id=1, source_target_pairs={{0,1},{1,0},{2,3},{3,2},{4,6},{5,7},{6,4},{7,5},{8,9},{9,8},{10,11... | collective-permute-start | bytes 1572872 | tf_op jit(solution)/shard_map/ppermute | solution.py:66
  3.7 1.2 reduce_sum.9
  4.9 2.0 %collective-permute-start.3 = (f32[2,256,256]{2,1,0:T(8,128)}, f32[2,256,256]{2,1,0:T(8,128)S(1)}, u32[]{:S(2)}, u32[]{:S(2)}) collective-permute-start(f32[2,256,256]{2,1,0:T(8,128)} %refs_0_.3), channel_id=1, source_target_pairs={{0,2},{1,3},{2,0},{3,1},{4,5},{5,4},{6,7},{7,6},{8,10},{9,11},{10,... | collective-permute-start | bytes 1572872 | tf_op jit(solution)/shard_map/ppermute | solution.py:66
  6.9 1.6 %collective-permute-start.12 = (f32[128,1024]{1,0:T(8,128)}, f32[128,1024]{1,0:T(8,128)S(1)}, u32[]{:S(2)}, u32[]{:S(2)}) collective-permute-start(f32[128,1024]{1,0:T(8,128)} %refs_4_.1), channel_id=1, source_target_pairs={{0,8},{1,9},{2,10},{3,11},{4,20},{5,21},{6,22},{7,23},{8,0},{9,1},... | collective-permute-start | bytes 1572872 | tf_op jit(solution)/shard_map/ppermute | solution.py:66
  8.5 6.3 %collective-permute-done = f32[8,128]{1,0:T(8,128)S(1)} collective-permute-done((f32[8,128]{1,0:T(8,128)S(1)}, f32[8,128]{1,0:T(8,128)S(1)}, u32[]{:S(2)}, u32[]{:S(2)}) %collective-permute-start) | collective-permute-done | bytes 4128 | tf_op jit(solution)/shard_map/ppermute | solution.py:66
  14.8 2.4 %collective-permute-start.1 = (f32[8,128]{1,0:T(8,128)S(1)}, f32[8,128]{1,0:T(8,128)S(1)}, u32[]{:S(2)}, u32[]{:S(2)}) collective-permute-start(f32[8,128]{1,0:T(8,128)S(1)} %broadcast_add_fusion), channel_id=1, source_target_pairs={{0,2},{1,3},{2,0},{3,1},{4,5},{5,4},{6,7},{7,6},{8,10},{9,11},{10,... | collective-permute-start | bytes 12296 | tf_op jit(solution)/shard_map/ppermute | solution.py:66
  17.2 1.5 %collective-permute-start.15 = (f32[128,1024]{1,0:T(8,128)}, f32[128,1024]{1,0:T(8,128)S(1)}, u32[]{:S(2)}, u32[]{:S(2)}) collective-permute-start(f32[128,1024]{1,0:T(8,128)} %refs_4_.1), channel_id=1, source_target_pairs={{0,1},{1,0},{2,3},{3,2},{4,6},{5,7},{6,4},{7,5},{8,9},{9,8},{10,11... | collective-permute-start | bytes 1572872 | tf_op jit(solution)/shard_map/ppermute | solution.py:66
  18.9 3.1 %collective-permute-start.13 = (f32[128,1024]{1,0:T(8,128)}, f32[128,1024]{1,0:T(8,128)S(1)}, u32[]{:S(2)}, u32[]{:S(2)}) collective-permute-start(f32[128,1024]{1,0:T(8,128)} %refs_4_.1), channel_id=1, source_target_pairs={{0,16},{1,17},{2,18},{3,19},{4,12},{5,13},{6,14},{7,15},{8,24},{9,... | collective-permute-start | bytes 1572872 | tf_op jit(solution)/shard_map/ppermute | solution.py:66
  21.9 1.5 %collective-permute-start.19 = (f32[128,1024]{1,0:T(8,128)}, f32[128,1024]{1,0:T(8,128)S(1)}, u32[]{:S(2)}, u32[]{:S(2)}) collective-permute-start(f32[128,1024]{1,0:T(8,128)} %refs_4_.1), channel_id=1, source_target_pairs={{0,2},{1,3},{2,0},{3,1},{4,5},{5,4},{6,7},{7,6},{8,10},{9,11},{10,... | collective-permute-start | bytes 1572872 | tf_op jit(solution)/shard_map/ppermute | solution.py:66
  24.1 7.7 %collective-permute-done.15.refs_8_ = f32[128,1024]{1,0:T(8,128)S(1)} collective-permute-done((f32[128,1024]{1,0:T(8,128)}, f32[128,1024]{1,0:T(8,128)S(1)}, u32[]{:S(2)}, u32[]{:S(2)}) %collective-permute-start.15) | collective-permute-done | bytes 524320 | tf_op jit(solution)/shard_map/ppermute | solution.py:66
  31.8 2.6 %collective-permute-start.14 = (f32[128,1024]{1,0:T(8,128)S(1)}, f32[128,1024]{1,0:T(8,128)S(1)}, u32[]{:S(2)}, u32[]{:S(2)}) collective-permute-start(f32[128,1024]{1,0:T(8,128)S(1)} %collective-permute-done.12.refs_5_), channel_id=1, source_target_pairs={{0,16},{1,17},{2,18},{3,19},{4,12},{5,13},{6,14},{7,15},{8,24},{9,... | collective-permute-start | bytes 1572872 | tf_op jit(solution)/shard_map/ppermute | solution.py:66
  34.6 1.5 %collective-permute-start.16 = (f32[128,1024]{1,0:T(8,128)S(1)}, f32[128,1024]{1,0:T(8,128)S(1)}, u32[]{:S(2)}, u32[]{:S(2)}) collective-permute-start(f32[128,1024]{1,0:T(8,128)S(1)} %collective-permute-done.12.refs_5_), channel_id=1, source_target_pairs={{0,1},{1,0},{2,3},{3,2},{4,6},{5,7},{6,4},{7,5},{8,9},{9,8},{10,11... | collective-permute-start | bytes 1572872 | tf_op jit(solution)/shard_map/ppermute | solution.py:66
  36.1 1.5 %collective-permute-start.20 = (f32[128,1024]{1,0:T(8,128)S(1)}, f32[128,1024]{1,0:T(8,128)S(1)}, u32[]{:S(2)}, u32[]{:S(2)}) collective-permute-start(f32[128,1024]{1,0:T(8,128)S(1)} %collective-permute-done.12.refs_5_), channel_id=1, source_target_pairs={{0,2},{1,3},{2,0},{3,1},{4,5},{5,4},{6,7},{7,6},{8,10},{9,11},{10,... | collective-permute-start | bytes 1572872 | tf_op jit(solution)/shard_map/ppermute | solution.py:66
  37.6 3.3 %collective-permute-start.17 = (f32[128,1024]{1,0:T(8,128)S(1)}, f32[128,1024]{1,0:T(8,128)S(1)}, u32[]{:S(2)}, u32[]{:S(2)}) collective-permute-start(f32[128,1024]{1,0:T(8,128)S(1)} %collective-permute-done.15.refs_8_), channel_id=1, source_target_pairs={{0,16},{1,17},{2,18},{3,19},{4,12},{5,13},{6,14},{7,15},{8,24},{9,... | collective-permute-start | bytes 1572872 | tf_op jit(solution)/shard_map/ppermute | solution.py:66
  41.0 5.7 %collective-permute-done.14.refs_7_ = f32[128,1024]{1,0:T(8,128)S(1)} collective-permute-done((f32[128,1024]{1,0:T(8,128)S(1)}, f32[128,1024]{1,0:T(8,128)S(1)}, u32[]{:S(2)}, u32[]{:S(2)}) %collective-permute-start.14) | collective-permute-done | bytes 524320 | tf_op jit(solution)/shard_map/ppermute | solution.py:66
  46.7 2.4 %collective-permute-done.16.refs_9_ = f32[128,1024]{1,0:T(8,128)S(1)} collective-permute-done((f32[128,1024]{1,0:T(8,128)S(1)}, f32[128,1024]{1,0:T(8,128)S(1)}, u32[]{:S(2)}, u32[]{:S(2)}) %collective-permute-start.16) | collective-permute-done | bytes 524320 | tf_op jit(solution)/shard_map/ppermute | solution.py:66
  49.2 1.5 %copy-done = f32[1024,256]{1,0:T(8,128)S(1)} copy-done((f32[1024,256]{1,0:T(8,128)S(1)}, f32[1024,256]{1,0:T(8,128)}, u32[]{:S(2)}) %copy-start) | copy-done | bytes 1048600
  50.7 1.0 copy-done.2
  51.8 1.4 project.1
  53.2 5.5 %collective-permute-done.17.refs_10_ = f32[128,1024]{1,0:T(8,128)S(1)} collective-permute-done((f32[128,1024]{1,0:T(8,128)S(1)}, f32[128,1024]{1,0:T(8,128)S(1)}, u32[]{:S(2)}, u32[]{:S(2)}) %collective-permute-start.17) | collective-permute-done | bytes 524320 | tf_op jit(solution)/shard_map/ppermute | solution.py:66
  60.0 1.5 %collective-permute-start.18 = (f32[128,1024]{1,0:T(8,128)S(1)}, f32[128,1024]{1,0:T(8,128)}, u32[]{:S(2)}, u32[]{:S(2)}) collective-permute-start(f32[128,1024]{1,0:T(8,128)S(1)} %collective-permute-done.14.refs_7_), channel_id=1, source_target_pairs={{0,1},{1,0},{2,3},{3,2},{4,6},{5,7},{6,4},{7,5},{8,9},{9,8},{10,11... | collective-permute-start | bytes 1572872 | tf_op jit(solution)/shard_map/ppermute | solution.py:66
  61.5 1.5 %collective-permute-start.22 = (f32[128,1024]{1,0:T(8,128)S(1)}, f32[128,1024]{1,0:T(8,128)}, u32[]{:S(2)}, u32[]{:S(2)}) collective-permute-start(f32[128,1024]{1,0:T(8,128)S(1)} %collective-permute-done.14.refs_7_), channel_id=1, source_target_pairs={{0,2},{1,3},{2,0},{3,1},{4,5},{5,4},{6,7},{7,6},{8,10},{9,11},{10,... | collective-permute-start | bytes 1572872 | tf_op jit(solution)/shard_map/ppermute | solution.py:66
  63.0 1.0 collective-permute-start.6
  64.0 9.9 %collective-permute-done.35.refs_1_ = f32[128,1024]{1,0:T(8,128)S(1)} collective-permute-done((f32[128,1024]{1,0:T(8,128)S(1)}, f32[128,1024]{1,0:T(8,128)S(1)}, u32[]{:S(2)}, u32[]{:S(2)}) %collective-permute-start.35) | collective-permute-done | bytes 524320 | tf_op jit(solution)/shard_map/ppermute | solution.py:66
  73.9 0.9 collective-permute-done.18.refs_11_
  75.4 4.5 %collective-permute-done.22.refs_15_ = f32[128,1024]{1,0:T(8,128)} collective-permute-done((f32[128,1024]{1,0:T(8,128)S(1)}, f32[128,1024]{1,0:T(8,128)}, u32[]{:S(2)}, u32[]{:S(2)}) %collective-permute-start.22) | collective-permute-done | bytes 524320 | tf_op jit(solution)/shard_map/ppermute | solution.py:66
  79.9 0.8 copy-done.33
  80.8 0.6 collective-permute-start.36
  81.4 3.0 %collective-permute-start.37 = (f32[128,1024]{1,0:T(8,128)S(1)}, f32[128,1024]{1,0:T(8,128)S(1)}, u32[]{:S(2)}, u32[]{:S(2)}) collective-permute-start(f32[128,1024]{1,0:T(8,128)S(1)} %collective-permute-done.35.refs_1_), channel_id=1, source_target_pairs={{0,16},{1,17},{2,18},{3,19},{4,12},{5,13},{6,14},{7,15},{8,24},{9,... | collective-permute-start | bytes 1572872 | tf_op jit(solution)/shard_map/ppermute | solution.py:66
  84.3 7.8 %collective-permute-done.7 = f32[776,128]{1,0:T(8,128)S(1)} collective-permute-done((f32[776,128]{1,0:T(8,128)S(1)}, f32[776,128]{1,0:T(8,128)S(1)}, u32[]{:S(2)}, u32[]{:S(2)}) %collective-permute-start.7) | collective-permute-done | bytes 397344 | tf_op jit(solution)/shard_map/ppermute | solution.py:66
  92.8 0.7 collective-permute-start.38
  93.5 1.3 collective-permute-done.8.theirs_ref
  95.0 2.7 %update.1 = (f32[264,256]{1,0:T(8,128)S(1)}, f32[264,256]{1,0:T(8,128)}, f32[264,256]{1,0:T(8,128)}, f32[264,256]{1,0:T(8,128)}) custom-call(f32[1024,256]{1,0:T(8,128)S(1)} %copy-done, f32[2,256,256]{2,1,0:T(8,128)S(1)} %copy-done.1, f32[776,128]{1,0:T(8,128)S(1)} %add.28.mine_ref, f32[776,128]{1,0:T(8,128)S(1)} %collective-permute-done.8.theirs_ref, ...), custom_call_target="tpu_custom_call" | custom-call | flops 805306368 | bytes 4988928 | tf_op jit(solution)/shard_map/update/pallas_call | solution.py:155
  97.6 0.7 collective-permute-start.10
  98.3 5.8 %collective-permute-done.37.refs_3_ = f32[128,1024]{1,0:T(8,128)S(1)} collective-permute-done((f32[128,1024]{1,0:T(8,128)S(1)}, f32[128,1024]{1,0:T(8,128)S(1)}, u32[]{:S(2)}, u32[]{:S(2)}) %collective-permute-start.37) | collective-permute-done | bytes 524320 | tf_op jit(solution)/shard_map/ppermute | solution.py:66
  104.2 0.8 collective-permute-start.11
  105.0 0.8 copy-done.43
  105.8 1.2 collective-permute-start.9
  107.1 1.5 %collective-permute-done.10.refs_2_ = f32[264,256]{1,0:T(8,128)S(1)} collective-permute-done((f32[264,256]{1,0:T(8,128)}, f32[264,256]{1,0:T(8,128)S(1)}, u32[]{:S(2)}, u32[]{:S(2)}) %collective-permute-start.10) | collective-permute-done | bytes 270368 | tf_op jit(solution)/shard_map/ppermute | solution.py:66
  108.6 3.3 %collective-permute-done.11.refs_3_ = f32[264,256]{1,0:T(8,128)} collective-permute-done((f32[264,256]{1,0:T(8,128)}, f32[264,256]{1,0:T(8,128)}, u32[]{:S(2)}, u32[]{:S(2)}) %collective-permute-start.11) | collective-permute-done | bytes 270368 | tf_op jit(solution)/shard_map/ppermute | solution.py:66
  111.9 1.9 %collective-permute-done.9.refs_1_ = f32[264,256]{1,0:T(8,128)} collective-permute-done((f32[264,256]{1,0:T(8,128)}, f32[264,256]{1,0:T(8,128)}, u32[]{:S(2)}, u32[]{:S(2)}) %collective-permute-start.9) | collective-permute-done | bytes 270368 | tf_op jit(solution)/shard_map/ppermute | solution.py:66
  114.0 1.3 fusion.1
  115.3 1.0 copy-done.6
  116.3 1.0 copy-done.8
  117.4 1.0 copy-done.10
  118.4 1.0 copy-done.12
  119.4 1.0 copy-done.14
  120.5 1.0 copy-done.16
  121.5 1.0 copy-done.18
  122.6 1.0 copy-done.20
  123.6 1.0 copy-done.22
  124.6 1.0 copy-done.24
  125.7 1.0 copy-done.26
  126.7 1.0 copy-done.28
  127.8 1.0 copy-done.30
  128.8 1.0 copy-done.32
  129.9 1.0 copy-done.34
  130.9 1.0 copy-done.36
  131.9 1.0 copy-done.38
  133.0 1.0 copy-done.40
  134.0 1.0 copy-done.42
  135.1 1.0 copy-done.44
  136.1 8.5 %shard_map.59 = (f32[256,4096]{1,0:T(8,128)}, bf16[512,1024]{1,0:T(8,128)(2,1)S(1)}) custom-call(f32[264,256]{1,0:T(8,128)S(1)} %get-tuple-element.12.refs_0_, f32[264,256]{1,0:T(8,128)} %collective-permute-done.9.refs_1_, f32[264,256]{1,0:T(8,128)S(1)} %collective-permute-done.10.refs_2_, f32[264,256]{1,0:T(8,128)} %collective-permute-done.11.refs_3_, ...), custom_call_target="tpu_custom_call" | custom-call | flops 4831838208 | bytes 15728640 | tf_op jit(solution)/shard_map/pallas_call | solution.py:236
  144.7 3.3 %shard_map.60 = f32[256,4096]{1,0:T(8,128)} custom-call(bf16[512,1024]{1,0:T(8,128)(2,1)S(1)} %get-tuple-element.16.refs_0_, f32[128,1024]{1,0:T(8,128)S(1)} %collective-permute-done.35.refs_1_, f32[128,1024]{1,0:T(8,128)S(1)} %collective-permute-done.36.refs_2_, f32[128,1024]{1,0:T(8,128)S(1)} %collective-permute-done.37.refs_3_, ...), custom_call_target="tpu_custom_call", output_to_operand_aliasing={{}: (9, {})} | custom-call | flops 1610612736 | bytes 5242880 | tf_op jit(solution)/shard_map/pallas_call | solution.py:236
  (124 shorter events, 4.2 us)
Async XLA Ops:
  0.6 21.3 %collective-permute-start.2 = (f32[2,256,256]{2,1,0:T(8,128)}, f32[2,256,256]{2,1,0:T(8,128)S(1)}, u32[]{:S(2)}, u32[]{:S(2)}) collective-permute-start(f32[2,256,256]{2,1,0:T(8,128)} %refs_0_.3), channel_id=1, source_target_pairs={{0,1},{1,0},{2,3},{3,2},{4,6},{5,7},{6,4},{7,5},{8,9},{9,8},{10,11... | collective-permute-start | bytes 1572872 | tf_op jit(solution)/shard_map/ppermute | solution.py:66
  4.8 10.0 %collective-permute-start = (f32[8,128]{1,0:T(8,128)S(1)}, f32[8,128]{1,0:T(8,128)S(1)}, u32[]{:S(2)}, u32[]{:S(2)}) collective-permute-start(f32[8,128]{1,0:T(8,128)S(1)} %broadcast_in_dim.2), channel_id=1, source_target_pairs={{0,1},{1,0},{2,3},{3,2},{4,6},{5,7},{6,4},{7,5},{8,9},{9,8},{10,11... | collective-permute-start | bytes 12296 | tf_op jit(solution)/shard_map/ppermute | solution.py:66
  4.9 18.6 %collective-permute-start.3 = (f32[2,256,256]{2,1,0:T(8,128)}, f32[2,256,256]{2,1,0:T(8,128)S(1)}, u32[]{:S(2)}, u32[]{:S(2)}) collective-permute-start(f32[2,256,256]{2,1,0:T(8,128)} %refs_0_.3), channel_id=1, source_target_pairs={{0,2},{1,3},{2,0},{3,1},{4,5},{5,4},{6,7},{7,6},{8,10},{9,11},{10,... | collective-permute-start | bytes 1572872 | tf_op jit(solution)/shard_map/ppermute | solution.py:66
  6.9 16.5 %collective-permute-start.12 = (f32[128,1024]{1,0:T(8,128)}, f32[128,1024]{1,0:T(8,128)S(1)}, u32[]{:S(2)}, u32[]{:S(2)}) collective-permute-start(f32[128,1024]{1,0:T(8,128)} %refs_4_.1), channel_id=1, source_target_pairs={{0,8},{1,9},{2,10},{3,11},{4,20},{5,21},{6,22},{7,23},{8,0},{9,1},... | collective-permute-start | bytes 1572872 | tf_op jit(solution)/shard_map/ppermute | solution.py:66
  14.8 4.0 %collective-permute-start.1 = (f32[8,128]{1,0:T(8,128)S(1)}, f32[8,128]{1,0:T(8,128)S(1)}, u32[]{:S(2)}, u32[]{:S(2)}) collective-permute-start(f32[8,128]{1,0:T(8,128)S(1)} %broadcast_add_fusion), channel_id=1, source_target_pairs={{0,2},{1,3},{2,0},{3,1},{4,5},{5,4},{6,7},{7,6},{8,10},{9,11},{10,... | collective-permute-start | bytes 12296 | tf_op jit(solution)/shard_map/ppermute | solution.py:66
  17.2 14.5 %collective-permute-start.15 = (f32[128,1024]{1,0:T(8,128)}, f32[128,1024]{1,0:T(8,128)S(1)}, u32[]{:S(2)}, u32[]{:S(2)}) collective-permute-start(f32[128,1024]{1,0:T(8,128)} %refs_4_.1), channel_id=1, source_target_pairs={{0,1},{1,0},{2,3},{3,2},{4,6},{5,7},{6,4},{7,5},{8,9},{9,8},{10,11... | collective-permute-start | bytes 1572872 | tf_op jit(solution)/shard_map/ppermute | solution.py:66
  18.9 15.7 %collective-permute-start.13 = (f32[128,1024]{1,0:T(8,128)}, f32[128,1024]{1,0:T(8,128)S(1)}, u32[]{:S(2)}, u32[]{:S(2)}) collective-permute-start(f32[128,1024]{1,0:T(8,128)} %refs_4_.1), channel_id=1, source_target_pairs={{0,16},{1,17},{2,18},{3,19},{4,12},{5,13},{6,14},{7,15},{8,24},{9,... | collective-permute-start | bytes 1572872 | tf_op jit(solution)/shard_map/ppermute | solution.py:66
  21.9 14.1 %collective-permute-start.19 = (f32[128,1024]{1,0:T(8,128)}, f32[128,1024]{1,0:T(8,128)S(1)}, u32[]{:S(2)}, u32[]{:S(2)}) collective-permute-start(f32[128,1024]{1,0:T(8,128)} %refs_4_.1), channel_id=1, source_target_pairs={{0,2},{1,3},{2,0},{3,1},{4,5},{5,4},{6,7},{7,6},{8,10},{9,11},{10,... | collective-permute-start | bytes 1572872 | tf_op jit(solution)/shard_map/ppermute | solution.py:66
  23.5 14.1 %collective-permute-start.23 = (f32[128,1024]{1,0:T(8,128)}, f32[128,1024]{1,0:T(8,128)S(1)}, u32[]{:S(2)}, u32[]{:S(2)}) collective-permute-start(f32[128,1024]{1,0:T(8,128)} %refs_4_.1), channel_id=1, source_target_pairs={{0,4},{1,5},{2,6},{3,7},{4,0},{5,1},{6,2},{7,3},{8,12},{9,13},{10,... | collective-permute-start | bytes 1572872 | tf_op jit(solution)/shard_map/ppermute | solution.py:66
  23.5 29.7 %copy-start.5 = (f32[128,1024]{1,0:T(8,128)}, f32[128,1024]{1,0:T(8,128)S(1)}, u32[]{:S(2)}) copy-start(f32[128,1024]{1,0:T(8,128)S(1)} %collective-permute-done.12.refs_5_) | copy-start | bytes 1572868
  23.5 17.5 %collective-permute-start.4 = (f32[2,256,256]{2,1,0:T(8,128)S(1)}, f32[2,256,256]{2,1,0:T(8,128)S(1)}, u32[]{:S(2)}, u32[]{:S(2)}) collective-permute-start(f32[2,256,256]{2,1,0:T(8,128)S(1)} %collective-permute-done.2.refs_1_), channel_id=1, source_target_pairs={{0,2},{1,3},{2,0},{3,1},{4,5},{5,4},{6,7},{7,6},{8,10},{9,11},{10,... | collective-permute-start | bytes 1572872 | tf_op jit(solution)/shard_map/ppermute | solution.py:66
  31.7 27.6 %copy-start.7 = (f32[128,1024]{1,0:T(8,128)}, f32[128,1024]{1,0:T(8,128)S(1)}, u32[]{:S(2)}) copy-start(f32[128,1024]{1,0:T(8,128)S(1)} %collective-permute-done.15.refs_8_) | copy-start | bytes 1572868
  31.8 14.9 %collective-permute-start.14 = (f32[128,1024]{1,0:T(8,128)S(1)}, f32[128,1024]{1,0:T(8,128)S(1)}, u32[]{:S(2)}, u32[]{:S(2)}) collective-permute-start(f32[128,1024]{1,0:T(8,128)S(1)} %collective-permute-done.12.refs_5_), channel_id=1, source_target_pairs={{0,16},{1,17},{2,18},{3,19},{4,12},{5,13},{6,14},{7,15},{8,24},{9,... | collective-permute-start | bytes 1572872 | tf_op jit(solution)/shard_map/ppermute | solution.py:66
  34.6 18.6 %copy-start.9 = (f32[128,1024]{1,0:T(8,128)}, f32[128,1024]{1,0:T(8,128)S(1)}, u32[]{:S(2)}) copy-start(f32[128,1024]{1,0:T(8,128)S(1)} %collective-permute-done.13.refs_6_) | copy-start | bytes 1572868
  34.6 14.5 %collective-permute-start.16 = (f32[128,1024]{1,0:T(8,128)S(1)}, f32[128,1024]{1,0:T(8,128)S(1)}, u32[]{:S(2)}, u32[]{:S(2)}) collective-permute-start(f32[128,1024]{1,0:T(8,128)S(1)} %collective-permute-done.12.refs_5_), channel_id=1, source_target_pairs={{0,1},{1,0},{2,3},{3,2},{4,6},{5,7},{6,4},{7,5},{8,9},{9,8},{10,11... | collective-permute-start | bytes 1572872 | tf_op jit(solution)/shard_map/ppermute | solution.py:66
  36.1 22.7 %copy-start.11 = (f32[128,1024]{1,0:T(8,128)}, f32[128,1024]{1,0:T(8,128)S(1)}, u32[]{:S(2)}) copy-start(f32[128,1024]{1,0:T(8,128)S(1)} %collective-permute-done.19.refs_12_) | copy-start | bytes 1572868
  36.1 13.0 %collective-permute-start.20 = (f32[128,1024]{1,0:T(8,128)S(1)}, f32[128,1024]{1,0:T(8,128)S(1)}, u32[]{:S(2)}, u32[]{:S(2)}) collective-permute-start(f32[128,1024]{1,0:T(8,128)S(1)} %collective-permute-done.12.refs_5_), channel_id=1, source_target_pairs={{0,2},{1,3},{2,0},{3,1},{4,5},{5,4},{6,7},{7,6},{8,10},{9,11},{10,... | collective-permute-start | bytes 1572872 | tf_op jit(solution)/shard_map/ppermute | solution.py:66
  37.6 15.6 %copy-start.13 = (f32[128,1024]{1,0:T(8,128)}, f32[128,1024]{1,0:T(8,128)S(1)}, u32[]{:S(2)}) copy-start(f32[128,1024]{1,0:T(8,128)S(1)} %collective-permute-done.23.refs_16_) | copy-start | bytes 1572868
  37.6 21.2 %collective-permute-start.17 = (f32[128,1024]{1,0:T(8,128)S(1)}, f32[128,1024]{1,0:T(8,128)S(1)}, u32[]{:S(2)}, u32[]{:S(2)}) collective-permute-start(f32[128,1024]{1,0:T(8,128)S(1)} %collective-permute-done.15.refs_8_), channel_id=1, source_target_pairs={{0,16},{1,17},{2,18},{3,19},{4,12},{5,13},{6,14},{7,15},{8,24},{9,... | collective-permute-start | bytes 1572872 | tf_op jit(solution)/shard_map/ppermute | solution.py:66
  41.0 17.8 %collective-permute-start.24 = (f32[128,1024]{1,0:T(8,128)S(1)}, f32[128,1024]{1,0:T(8,128)S(1)}, u32[]{:S(2)}, u32[]{:S(2)}) collective-permute-start(f32[128,1024]{1,0:T(8,128)S(1)} %collective-permute-done.12.refs_5_), channel_id=1, source_target_pairs={{0,4},{1,5},{2,6},{3,7},{4,0},{5,1},{6,2},{7,3},{8,12},{9,13},{10,... | collective-permute-start | bytes 1572872 | tf_op jit(solution)/shard_map/ppermute | solution.py:66
  46.7 17.3 %copy-start.15 = (f32[128,1024]{1,0:T(8,128)}, f32[128,1024]{1,0:T(8,128)S(1)}, u32[]{:S(2)}) copy-start(f32[128,1024]{1,0:T(8,128)S(1)} %collective-permute-done.14.refs_7_) | copy-start | bytes 1572868
  46.7 13.3 %collective-permute-start.31 = (f32[128,1024]{1,0:T(8,128)S(1)}, f32[128,1024]{1,0:T(8,128)S(1)}, u32[]{:S(2)}, u32[]{:S(2)}) collective-permute-start(f32[128,1024]{1,0:T(8,128)S(1)} %collective-permute-done.15.refs_8_), channel_id=1, source_target_pairs={{0,4},{1,5},{2,6},{3,7},{4,0},{5,1},{6,2},{7,3},{8,12},{9,13},{10,... | collective-permute-start | bytes 1572872 | tf_op jit(solution)/shard_map/ppermute | solution.py:66
  49.1 31.7 %copy-start.17 = (f32[128,1024]{1,0:T(8,128)}, f32[128,1024]{1,0:T(8,128)S(1)}, u32[]{:S(2)}) copy-start(f32[128,1024]{1,0:T(8,128)S(1)} %collective-permute-done.16.refs_9_) | copy-start | bytes 1572868
  49.1 10.3 %collective-permute-start.21 = (f32[128,1024]{1,0:T(8,128)S(1)}, f32[128,1024]{1,0:T(8,128)S(1)}, u32[]{:S(2)}, u32[]{:S(2)}) collective-permute-start(f32[128,1024]{1,0:T(8,128)S(1)} %collective-permute-done.13.refs_6_), channel_id=1, source_target_pairs={{0,2},{1,3},{2,0},{3,1},{4,5},{5,4},{6,7},{7,6},{8,10},{9,11},{10,... | collective-permute-start | bytes 1572872 | tf_op jit(solution)/shard_map/ppermute | solution.py:66
  49.1 25.7 %copy-start.19 = (f32[128,1024]{1,0:T(8,128)}, f32[128,1024]{1,0:T(8,128)S(1)}, u32[]{:S(2)}) copy-start(f32[128,1024]{1,0:T(8,128)S(1)} %collective-permute-done.20.refs_13_) | copy-start | bytes 1572868
  49.1 13.9 %collective-permute-start.25 = (f32[128,1024]{1,0:T(8,128)S(1)}, f32[128,1024]{1,0:T(8,128)S(1)}, u32[]{:S(2)}, u32[]{:S(2)}) collective-permute-start(f32[128,1024]{1,0:T(8,128)S(1)} %collective-permute-done.13.refs_6_), channel_id=1, source_target_pairs={{0,4},{1,5},{2,6},{3,7},{4,0},{5,1},{6,2},{7,3},{8,12},{9,13},{10,... | collective-permute-start | bytes 1572872 | tf_op jit(solution)/shard_map/ppermute | solution.py:66
  51.7 43.2 %copy-start.1 = (f32[2,256,256]{2,1,0:T(8,128)S(1)}, f32[2,256,256]{2,1,0:T(8,128)}, u32[]{:S(2)}) copy-start(f32[2,256,256]{2,1,0:T(8,128)} %factors_ref.1) | copy-start | bytes 1572868
  51.8 43.2 %copy-start.3 = (f32[2,256,256]{2,1,0:T(8,128)S(1)}, f32[2,256,256]{2,1,0:T(8,128)}, u32[]{:S(2)}) copy-start(f32[2,256,256]{2,1,0:T(8,128)} %refs_0_.3) | copy-start | bytes 1572868
  53.2 62.0 %copy-start.4 = (f32[128,1024]{1,0:T(8,128)S(1)}, f32[128,1024]{1,0:T(8,128)}, u32[]{:S(2)}) copy-start(f32[128,1024]{1,0:T(8,128)} %refs_4_.1) | copy-start | bytes 1572868
  58.8 45.4 %copy-start.21 = (f32[128,1024]{1,0:T(8,128)}, f32[128,1024]{1,0:T(8,128)S(1)}, u32[]{:S(2)}) copy-start(f32[128,1024]{1,0:T(8,128)S(1)} %collective-permute-done.17.refs_10_) | copy-start | bytes 1572868
  58.8 2.7 %collective-permute-start.5 = (f32[776,128]{1,0:T(8,128)S(1)}, f32[776,128]{1,0:T(8,128)S(1)}, u32[]{:S(2)}, u32[]{:S(2)}) collective-permute-start(f32[776,128]{1,0:T(8,128)S(1)} %get-tuple-element.11), channel_id=1, source_target_pairs={{0,4},{1,5},{2,6},{3,7},{4,0},{5,1},{6,2},{7,3},{8,12},{9,13},{10,... | collective-permute-start | bytes 1191944 | tf_op jit(solution)/shard_map/ppermute | solution.py:66
  58.8 45.4 %copy-start.23 = (f32[128,1024]{1,0:T(8,128)}, f32[128,1024]{1,0:T(8,128)S(1)}, u32[]{:S(2)}) copy-start(f32[128,1024]{1,0:T(8,128)S(1)} %collective-permute-done.24.refs_17_) | copy-start | bytes 1572868
  58.8 5.2 %collective-permute-start.27 = (f32[128,1024]{1,0:T(8,128)S(1)}, f32[128,1024]{1,0:T(8,128)S(1)}, u32[]{:S(2)}, u32[]{:S(2)}) collective-permute-start(f32[128,1024]{1,0:T(8,128)S(1)} %collective-permute-done.19.refs_12_), channel_id=1, source_target_pairs={{0,4},{1,5},{2,6},{3,7},{4,0},{5,1},{6,2},{7,3},{8,12},{9,13},{10,... | collective-permute-start | bytes 1572872 | tf_op jit(solution)/shard_map/ppermute | solution.py:66
  59.4 45.6 %copy-start.27 = (f32[128,1024]{1,0:T(8,128)}, f32[128,1024]{1,0:T(8,128)S(1)}, u32[]{:S(2)}) copy-start(f32[128,1024]{1,0:T(8,128)S(1)} %collective-permute-done.21.refs_14_) | copy-start | bytes 1572868
  59.4 14.6 %collective-permute-start.35 = (f32[128,1024]{1,0:T(8,128)S(1)}, f32[128,1024]{1,0:T(8,128)S(1)}, u32[]{:S(2)}, u32[]{:S(2)}) collective-permute-start(f32[128,1024]{1,0:T(8,128)S(1)} %collective-permute-done.15.refs_8_), channel_id=1, source_target_pairs={{0,2},{1,3},{2,0},{3,1},{4,5},{5,4},{6,7},{7,6},{8,10},{9,11},{10,... | collective-permute-start | bytes 1572872 | tf_op jit(solution)/shard_map/ppermute | solution.py:66
  60.0 45.0 %copy-start.25 = (f32[128,1024]{1,0:T(8,128)}, f32[128,1024]{1,0:T(8,128)S(1)}, u32[]{:S(2)}) copy-start(f32[128,1024]{1,0:T(8,128)S(1)} %collective-permute-done.31.refs_24_) | copy-start | bytes 1572868
  60.0 14.9 %collective-permute-start.18 = (f32[128,1024]{1,0:T(8,128)S(1)}, f32[128,1024]{1,0:T(8,128)}, u32[]{:S(2)}, u32[]{:S(2)}) collective-permute-start(f32[128,1024]{1,0:T(8,128)S(1)} %collective-permute-done.14.refs_7_), channel_id=1, source_target_pairs={{0,1},{1,0},{2,3},{3,2},{4,6},{5,7},{6,4},{7,5},{8,9},{9,8},{10,11... | collective-permute-start | bytes 1572872 | tf_op jit(solution)/shard_map/ppermute | solution.py:66
  61.5 18.5 %collective-permute-start.22 = (f32[128,1024]{1,0:T(8,128)S(1)}, f32[128,1024]{1,0:T(8,128)}, u32[]{:S(2)}, u32[]{:S(2)}) collective-permute-start(f32[128,1024]{1,0:T(8,128)S(1)} %collective-permute-done.14.refs_7_), channel_id=1, source_target_pairs={{0,2},{1,3},{2,0},{3,1},{4,5},{5,4},{6,7},{7,6},{8,10},{9,11},{10,... | collective-permute-start | bytes 1572872 | tf_op jit(solution)/shard_map/ppermute | solution.py:66
  63.0 42.8 %copy-start.29 = (f32[128,1024]{1,0:T(8,128)}, f32[128,1024]{1,0:T(8,128)S(1)}, u32[]{:S(2)}) copy-start(f32[128,1024]{1,0:T(8,128)S(1)} %collective-permute-done.25.refs_18_) | copy-start | bytes 1572868
  63.0 11.9 %collective-permute-start.6 = (f32[776,128]{1,0:T(8,128)S(1)}, f32[776,128]{1,0:T(8,128)S(1)}, u32[]{:S(2)}, u32[]{:S(2)}) collective-permute-start(f32[776,128]{1,0:T(8,128)S(1)} %add.26), channel_id=1, source_target_pairs={{0,8},{1,9},{2,10},{3,11},{4,20},{5,21},{6,22},{7,23},{8,0},{9,1},... | collective-permute-start | bytes 1191944 | tf_op jit(solution)/shard_map/ppermute | solution.py:66
  64.0 43.0 %copy-start.31 = (f32[128,1024]{1,0:T(8,128)}, f32[128,1024]{1,0:T(8,128)S(1)}, u32[]{:S(2)}) copy-start(f32[128,1024]{1,0:T(8,128)S(1)} %collective-permute-done.27.refs_20_) | copy-start | bytes 1572868
  64.0 16.0 %collective-permute-start.26 = (f32[128,1024]{1,0:T(8,128)S(1)}, f32[128,1024]{1,0:T(8,128)S(1)}, u32[]{:S(2)}, u32[]{:S(2)}) collective-permute-start(f32[128,1024]{1,0:T(8,128)S(1)} %collective-permute-done.14.refs_7_), channel_id=1, source_target_pairs={{0,4},{1,5},{2,6},{3,7},{4,0},{5,1},{6,2},{7,3},{8,12},{9,13},{10,... | collective-permute-start | bytes 1572872 | tf_op jit(solution)/shard_map/ppermute | solution.py:66
  73.9 6.8 %collective-permute-start.32 = (f32[128,1024]{1,0:T(8,128)S(1)}, f32[128,1024]{1,0:T(8,128)S(1)}, u32[]{:S(2)}, u32[]{:S(2)}) collective-permute-start(f32[128,1024]{1,0:T(8,128)S(1)} %collective-permute-done.16.refs_9_), channel_id=1, source_target_pairs={{0,4},{1,5},{2,6},{3,7},{4,0},{5,1},{6,2},{7,3},{8,12},{9,13},{10,... | collective-permute-start | bytes 1572872 | tf_op jit(solution)/shard_map/ppermute | solution.py:66
  74.9 6.5 %collective-permute-start.28 = (f32[128,1024]{1,0:T(8,128)S(1)}, f32[128,1024]{1,0:T(8,128)S(1)}, u32[]{:S(2)}, u32[]{:S(2)}) collective-permute-start(f32[128,1024]{1,0:T(8,128)S(1)} %collective-permute-done.20.refs_13_), channel_id=1, source_target_pairs={{0,4},{1,5},{2,6},{3,7},{4,0},{5,1},{6,2},{7,3},{8,12},{9,13},{10,... | collective-permute-start | bytes 1572872 | tf_op jit(solution)/shard_map/ppermute | solution.py:66
  74.9 17.3 %collective-permute-start.33 = (f32[128,1024]{1,0:T(8,128)S(1)}, f32[128,1024]{1,0:T(8,128)S(1)}, u32[]{:S(2)}, u32[]{:S(2)}) collective-permute-start(f32[128,1024]{1,0:T(8,128)S(1)} %collective-permute-done.17.refs_10_), channel_id=1, source_target_pairs={{0,4},{1,5},{2,6},{3,7},{4,0},{5,1},{6,2},{7,3},{8,12},{9,13},{10,... | collective-permute-start | bytes 1572872 | tf_op jit(solution)/shard_map/ppermute | solution.py:66
  79.9 12.2 %collective-permute-start.7 = (f32[776,128]{1,0:T(8,128)S(1)}, f32[776,128]{1,0:T(8,128)S(1)}, u32[]{:S(2)}, u32[]{:S(2)}) collective-permute-start(f32[776,128]{1,0:T(8,128)S(1)} %add.27), channel_id=1, source_target_pairs={{0,16},{1,17},{2,18},{3,19},{4,12},{5,13},{6,14},{7,15},{8,24},{9,... | collective-permute-start | bytes 1191944 | tf_op jit(solution)/shard_map/ppermute | solution.py:66
  80.7 12.0 %collective-permute-start.29 = (f32[128,1024]{1,0:T(8,128)S(1)}, f32[128,1024]{1,0:T(8,128)S(1)}, u32[]{:S(2)}, u32[]{:S(2)}) collective-permute-start(f32[128,1024]{1,0:T(8,128)S(1)} %collective-permute-done.21.refs_14_), channel_id=1, source_target_pairs={{0,4},{1,5},{2,6},{3,7},{4,0},{5,1},{6,2},{7,3},{8,12},{9,13},{10,... | collective-permute-start | bytes 1572872 | tf_op jit(solution)/shard_map/ppermute | solution.py:66
  80.8 26.2 %copy-start.35 = (f32[128,1024]{1,0:T(8,128)}, f32[128,1024]{1,0:T(8,128)S(1)}, u32[]{:S(2)}) copy-start(f32[128,1024]{1,0:T(8,128)S(1)} %collective-permute-done.32.refs_25_) | copy-start | bytes 1572868
  80.8 16.9 %collective-permute-start.36 = (f32[128,1024]{1,0:T(8,128)S(1)}, f32[128,1024]{1,0:T(8,128)S(1)}, u32[]{:S(2)}, u32[]{:S(2)}) collective-permute-start(f32[128,1024]{1,0:T(8,128)S(1)} %collective-permute-done.16.refs_9_), channel_id=1, source_target_pairs={{0,2},{1,3},{2,0},{3,1},{4,5},{5,4},{6,7},{7,6},{8,10},{9,11},{10,... | collective-permute-start | bytes 1572872 | tf_op jit(solution)/shard_map/ppermute | solution.py:66
  81.4 25.6 %copy-start.37 = (f32[128,1024]{1,0:T(8,128)}, f32[128,1024]{1,0:T(8,128)S(1)}, u32[]{:S(2)}) copy-start(f32[128,1024]{1,0:T(8,128)S(1)} %collective-permute-done.28.refs_21_) | copy-start | bytes 1572868
  81.4 22.8 %collective-permute-start.37 = (f32[128,1024]{1,0:T(8,128)S(1)}, f32[128,1024]{1,0:T(8,128)S(1)}, u32[]{:S(2)}, u32[]{:S(2)}) collective-permute-start(f32[128,1024]{1,0:T(8,128)S(1)} %collective-permute-done.35.refs_1_), channel_id=1, source_target_pairs={{0,16},{1,17},{2,18},{3,19},{4,12},{5,13},{6,14},{7,15},{8,24},{9,... | collective-permute-start | bytes 1572872 | tf_op jit(solution)/shard_map/ppermute | solution.py:66
  92.1 12.8 %collective-permute-start.34 = (f32[128,1024]{1,0:T(8,128)}, f32[128,1024]{1,0:T(8,128)S(1)}, u32[]{:S(2)}, u32[]{:S(2)}) collective-permute-start(f32[128,1024]{1,0:T(8,128)} %collective-permute-done.18.refs_11_), channel_id=1, source_target_pairs={{0,4},{1,5},{2,6},{3,7},{4,0},{5,1},{6,2},{7,3},{8,12},{9,13},{10,... | collective-permute-start | bytes 1572872 | tf_op jit(solution)/shard_map/ppermute | solution.py:66
  92.2 14.8 %copy-start.39 = (f32[128,1024]{1,0:T(8,128)}, f32[128,1024]{1,0:T(8,128)S(1)}, u32[]{:S(2)}) copy-start(f32[128,1024]{1,0:T(8,128)S(1)} %collective-permute-done.33.refs_26_) | copy-start | bytes 1572868
  92.2 2.6 %collective-permute-start.8 = (f32[776,128]{1,0:T(8,128)S(1)}, f32[776,128]{1,0:T(8,128)S(1)}, u32[]{:S(2)}, u32[]{:S(2)}) collective-permute-start(f32[776,128]{1,0:T(8,128)S(1)} %add.28.mine_ref), channel_id=1, source_target_pairs={{0,4},{1,5},{2,6},{3,7},{4,0},{5,1},{6,2},{7,3},{8,12},{9,13},{10,... | collective-permute-start | bytes 1191944 | tf_op jit(solution)/shard_map/ppermute | solution.py:66
  92.8 14.2 %copy-start.41 = (f32[128,1024]{1,0:T(8,128)}, f32[128,1024]{1,0:T(8,128)S(1)}, u32[]{:S(2)}) copy-start(f32[128,1024]{1,0:T(8,128)S(1)} %collective-permute-done.29.refs_22_) | copy-start | bytes 1572868
  92.8 14.2 %collective-permute-start.38 = (f32[128,1024]{1,0:T(8,128)}, f32[128,1024]{1,0:T(8,128)S(1)}, u32[]{:S(2)}, u32[]{:S(2)}) collective-permute-start(f32[128,1024]{1,0:T(8,128)} %collective-permute-done.18.refs_11_), channel_id=1, source_target_pairs={{0,2},{1,3},{2,0},{3,1},{4,5},{5,4},{6,7},{7,6},{8,10},{9,11},{10,... | collective-permute-start | bytes 1572872 | tf_op jit(solution)/shard_map/ppermute | solution.py:66
  94.8 20.5 %collective-permute-start.30 = (f32[128,1024]{1,0:T(8,128)}, f32[128,1024]{1,0:T(8,128)}, u32[]{:S(2)}, u32[]{:S(2)}) collective-permute-start(f32[128,1024]{1,0:T(8,128)} %collective-permute-done.22.refs_15_), channel_id=1, source_target_pairs={{0,4},{1,5},{2,6},{3,7},{4,0},{5,1},{6,2},{7,3},{8,12},{9,13},{10,... | collective-permute-start | bytes 1572872 | tf_op jit(solution)/shard_map/ppermute | solution.py:66
  97.6 11.0 %collective-permute-start.10 = (f32[264,256]{1,0:T(8,128)}, f32[264,256]{1,0:T(8,128)S(1)}, u32[]{:S(2)}, u32[]{:S(2)}) collective-permute-start(f32[264,256]{1,0:T(8,128)} %get-tuple-element.14), channel_id=1, source_target_pairs={{0,2},{1,3},{2,0},{3,1},{4,5},{5,4},{6,7},{7,6},{8,10},{9,11},{10,... | collective-permute-start | bytes 811016 | tf_op jit(solution)/shard_map/ppermute | solution.py:66
  104.2 7.8 %collective-permute-start.11 = (f32[264,256]{1,0:T(8,128)}, f32[264,256]{1,0:T(8,128)}, u32[]{:S(2)}, u32[]{:S(2)}) collective-permute-start(f32[264,256]{1,0:T(8,128)} %get-tuple-element.15), channel_id=1, source_target_pairs={{0,3},{1,2},{2,1},{3,0},{4,7},{5,6},{6,5},{7,4},{8,11},{9,10},{10,... | collective-permute-start | bytes 811016 | tf_op jit(solution)/shard_map/ppermute | solution.py:66
  105.8 8.1 %collective-permute-start.9 = (f32[264,256]{1,0:T(8,128)}, f32[264,256]{1,0:T(8,128)}, u32[]{:S(2)}, u32[]{:S(2)}) collective-permute-start(f32[264,256]{1,0:T(8,128)} %get-tuple-element.13), channel_id=1, source_target_pairs={{0,1},{1,0},{2,3},{3,2},{4,6},{5,7},{6,4},{7,5},{8,9},{9,8},{10,11... | collective-permute-start | bytes 811016 | tf_op jit(solution)/shard_map/ppermute | solution.py:66
  107.0 37.6 %collective-permute-start.39 = (f32[128,1024]{1,0:T(8,128)S(1)}, f32[128,1024]{1,0:T(8,128)S(1)}, u32[]{:S(2)}, u32[]{:S(2)}) collective-permute-start(f32[128,1024]{1,0:T(8,128)S(1)} %collective-permute-done.35.refs_1_), channel_id=1, source_target_pairs={{0,4},{1,5},{2,6},{3,7},{4,0},{5,1},{6,2},{7,3},{8,12},{9,13},{10,... | collective-permute-start | bytes 1572872 | tf_op jit(solution)/shard_map/ppermute | solution.py:66
  108.6 36.1 %collective-permute-start.40 = (f32[128,1024]{1,0:T(8,128)S(1)}, f32[128,1024]{1,0:T(8,128)S(1)}, u32[]{:S(2)}, u32[]{:S(2)}) collective-permute-start(f32[128,1024]{1,0:T(8,128)S(1)} %collective-permute-done.36.refs_2_), channel_id=1, source_target_pairs={{0,4},{1,5},{2,6},{3,7},{4,0},{5,1},{6,2},{7,3},{8,12},{9,13},{10,... | collective-permute-start | bytes 1572872 | tf_op jit(solution)/shard_map/ppermute | solution.py:66
  111.9 32.8 %collective-permute-start.41 = (f32[128,1024]{1,0:T(8,128)S(1)}, f32[128,1024]{1,0:T(8,128)S(1)}, u32[]{:S(2)}, u32[]{:S(2)}) collective-permute-start(f32[128,1024]{1,0:T(8,128)S(1)} %collective-permute-done.37.refs_3_), channel_id=1, source_target_pairs={{0,4},{1,5},{2,6},{3,7},{4,0},{5,1},{6,2},{7,3},{8,12},{9,13},{10,... | collective-permute-start | bytes 1572872 | tf_op jit(solution)/shard_map/ppermute | solution.py:66
  113.8 30.8 %collective-permute-start.42 = (f32[128,1024]{1,0:T(8,128)S(1)}, f32[128,1024]{1,0:T(8,128)S(1)}, u32[]{:S(2)}, u32[]{:S(2)}) collective-permute-start(f32[128,1024]{1,0:T(8,128)S(1)} %collective-permute-done.38.refs_4_), channel_id=1, source_target_pairs={{0,4},{1,5},{2,6},{3,7},{4,0},{5,1},{6,2},{7,3},{8,12},{9,13},{10,... | collective-permute-start | bytes 1572872 | tf_op jit(solution)/shard_map/ppermute | solution.py:66
  (24 other events, 25.0 us)

commit v3 on v2

--- a/solution.py
+++ b/solution.py
@@ -161,7 +161,7 @@
     )(basis, factors, mine, theirs, *vecs)
 
 
-def product(plan, b2, pieces, others, slots, base=None):
+def product(plan, b2, pieces, others, slots, lines, base=None):
     n_col, n_z = plan.n_col, plan.n_z
     blk, width = pieces[0][0].shape
     depth = blk * plan.n_row
@@ -178,7 +178,7 @@
         b, c = refs[:n_given], refs[n_given : n_given + 2 * half]
         rest = refs[n_given + 2 * half + len(more) :]
         if base is None:
-            out, both, cbuf, obuf, in_sem, out_sem = rest
+            out, both, wsum, cbuf, obuf, in_sem, out_sem = rest
         else:
             (both,), (out, cbuf, obuf, in_sem, out_sem) = b, rest
         z, core, col = plan.place()
@@ -209,6 +209,12 @@
             at = pl.multiple_of(plan.col_of(col, core, s) * kb, kb)
             both[:rows, pl.ds(at, kb)] = hi
             both[rows:, pl.ds(at, kb)] = lo
+        if base is None:
+            shares = [ref[rows : rows + lines, :] for ref in b]
+            shares = [pick(core, [shares[m.index(i)] for m in plan.col_masks]) for i in range(n_col)]
+            while len(shares) > 1:
+                shares = [shares[i] + shares[i + 1] for i in range(0, len(shares), 2)]
+            wsum[...] = shares[0] / jnp.sqrt(F32(width * n_col))
         for s in range(len(slots)):
             slot = s % 2
             if s + 1 < len(slots):
@@ -232,12 +238,13 @@
             store(s, s % 2).wait()
 
     anywhere, near = pl.BlockSpec(memory_space=pl.ANY), pl.BlockSpec(memory_space=pltpu.VMEM)
-    split, n_split = jax.ShapeDtypeStruct((2 * rows, depth), jnp.bfloat16), 1 if base is None else 0
+    extra = [jax.ShapeDtypeStruct((2 * rows, depth), jnp.bfloat16), jax.ShapeDtypeStruct((lines, kb), F32)]
+    extra = extra if base is None else []
     return pl.pallas_call(
         body,
-        out_shape=[jax.ShapeDtypeStruct((rows, width * n_col), F32)] + [split] * n_split,
+        out_shape=[jax.ShapeDtypeStruct((rows, width * n_col), F32)] + extra,
         in_specs=[near] * n_given + [anywhere] * len(flat + more),
-        out_specs=[anywhere] + [near] * n_split,
+        out_specs=[anywhere] + [near] * len(extra),
         scratch_shapes=[
             pltpu.VMEM((2, depth, width), F32),
             pltpu.VMEM((2, rows, width), F32),
@@ -262,9 +269,8 @@
 
     def per_device(basis, coef, panels, factors):
         nb, kb = panels.shape[2], basis.shape[1]
-        part = panels.shape[1]
         n_col, z_bits = plan.n_col, plan.z_bits
-        _, core, _ = plan.place()
+        z, core, col = plan.place()
 
         vecs = spread(plan, panels)
         sums = jnp.broadcast_to(jnp.sum(coef, axis=1)[None, :], (8, coef.shape[0]))
@@ -289,15 +295,11 @@
         sends = update(plan, basis, vecs, factors, mine, theirs)
 
         tall = [sends[0]] + [plan.over_col(sends[s], s) for s in range(1, n_col)]
-        shares = [x[part : part + 2 * nb // kb].reshape(2, nb) for x in tall]
-        by_mask = [pick(core, [shares[m.index(i)] for m in plan.col_masks]) for i in range(n_col)]
-        while len(by_mask) > 1:
-            by_mask = [by_mask[i] + by_mask[i + 1] for i in range(0, len(by_mask), 2)]
-        wsum = by_mask[0] / jnp.sqrt(F32(coef.shape[1] * n_col))
+        lines = 2 * nb // kb
         first = list(range(n_col - 1))
-        held = product(plan, tall, pieces, others, first)
-        (vectors,) = product(plan, (), pieces, others, [n_col - 1], held)
-        return vectors, wsum
+        *held, wsum = product(plan, tall, pieces, others, first, lines)
+        (vectors,) = product(plan, (), pieces, others, [n_col - 1], lines, held)
+        return vectors, wsum.reshape(2, nb)
 
     placed = (P("row", "col"), P("row", "col"), P(None, ("row", "col"), None), P())
     return jax.shard_map(

time: 149 us -> 138 us (0.926)
  local copies, waits for them, and re-layouts: 25 us -> 2.28 us
  waiting for transfers between devices: 65 us -> 83.6 us
  starting transfers between devices: 38.4 us -> 34 us
    unnamed x90 -> x10, local copies, waits for them, and re-layouts: 25 us -> 2.28 us
    ppermute x43, waiting for transfers between devices: 65 us -> 83.6 us  [permute(): return lax.ppermute(x, BOTH, pairs)]
    ppermute x43, starting transfers between devices: 38.4 us -> 34 us  [permute(): return lax.ppermute(x, BOTH, pairs)]
  transfers between devices with their start and end apart: 43 -> 43, of which waited for: 17 -> 15; matrix products, arithmetic and copies ran while one was open for 2% -> 1% of each run, Pallas kernels for 9% -> 8%
where the time goes in v3:
time: 138 us; the launch traced here: 137 us
  waiting for transfers between devices  83.6 us (61%)
  starting transfers between devices  34 us (25%)
  Pallas kernels  14.8 us (11%)
  local copies, waits for them, and re-layouts  2.28 us (2%)
    ppermute x43, waiting for transfers between devices, permute(): return lax.ppermute(x, BOTH, pairs)  83.6 us
    ppermute x43, starting transfers between devices, permute(): return lax.ppermute(x, BOTH, pairs)  34 us
    pallas_call x2, Pallas kernels, product(): pl.pallas_call(body, out_shape=[jax.ShapeDtypeStruct((rows, width * n_col...  11.5 us
  transfers between devices with their start and end apart: 43, of which 15 were waited for; matrix products, arithmetic and copies ran while one was open for 1% of the time, Pallas kernels for 8%

profile of v3, /device:TPU:0, one launch (start us, length us, event | category | flops | bytes accessed | tf_op | source)
XLA Modules:
  0.0 137.0 jit_solution(4529244722150929406)
XLA Ops:
  0.6 3.0 %collective-permute-start.2 = (f32[2,256,256]{2,1,0:T(8,128)}, f32[2,256,256]{2,1,0:T(8,128)S(1)}, u32[]{:S(2)}, u32[]{:S(2)}) collective-permute-start(f32[2,256,256]{2,1,0:T(8,128)} %refs_0_.3), channel_id=1, source_target_pairs={{0,1},{1,0},{2,3},{3,2},{4,6},{5,7},{6,4},{7,5},{8,9},{9,8},{10,11... | collective-permute-start | bytes 1572872 | tf_op jit(solution)/shard_map/ppermute | solution.py:66
  3.7 1.5 %collective-permute-start.3 = (f32[2,256,256]{2,1,0:T(8,128)}, f32[2,256,256]{2,1,0:T(8,128)S(1)}, u32[]{:S(2)}, u32[]{:S(2)}) collective-permute-start(f32[2,256,256]{2,1,0:T(8,128)} %refs_0_.3), channel_id=1, source_target_pairs={{0,2},{1,3},{2,0},{3,1},{4,5},{5,4},{6,7},{7,6},{8,10},{9,11},{10,... | collective-permute-start | bytes 1572872 | tf_op jit(solution)/shard_map/ppermute | solution.py:66
  5.2 1.6 %collective-permute-start.12 = (f32[128,1024]{1,0:T(8,128)}, f32[128,1024]{1,0:T(8,128)S(1)}, u32[]{:S(2)}, u32[]{:S(2)}) collective-permute-start(f32[128,1024]{1,0:T(8,128)} %refs_4_.1), channel_id=1, source_target_pairs={{0,8},{1,9},{2,10},{3,11},{4,20},{5,21},{6,22},{7,23},{8,0},{9,1},... | collective-permute-start | bytes 1572872 | tf_op jit(solution)/shard_map/ppermute | solution.py:66
  6.8 0.5 collective-permute-start.15
  7.3 1.2 reduce_sum.9
  8.5 1.6 %collective-permute-start = (f32[8,128]{1,0:T(8,128)S(1)}, f32[8,128]{1,0:T(8,128)S(1)}, u32[]{:S(2)}, u32[]{:S(2)}) collective-permute-start(f32[8,128]{1,0:T(8,128)S(1)} %broadcast_in_dim.2), channel_id=1, source_target_pairs={{0,1},{1,0},{2,3},{3,2},{4,6},{5,7},{6,4},{7,5},{8,9},{9,8},{10,11... | collective-permute-start | bytes 12296 | tf_op jit(solution)/shard_map/ppermute | solution.py:66
  10.0 6.1 %collective-permute-done.2.refs_1_ = f32[2,256,256]{2,1,0:T(8,128)S(1)} collective-permute-done((f32[2,256,256]{2,1,0:T(8,128)}, f32[2,256,256]{2,1,0:T(8,128)S(1)}, u32[]{:S(2)}, u32[]{:S(2)}) %collective-permute-start.2) | collective-permute-done | bytes 524320 | tf_op jit(solution)/shard_map/ppermute | solution.py:66
  16.2 1.5 %collective-permute-start.4 = (f32[2,256,256]{2,1,0:T(8,128)S(1)}, f32[2,256,256]{2,1,0:T(8,128)S(1)}, u32[]{:S(2)}, u32[]{:S(2)}) collective-permute-start(f32[2,256,256]{2,1,0:T(8,128)S(1)} %collective-permute-done.2.refs_1_), channel_id=1, source_target_pairs={{0,2},{1,3},{2,0},{3,1},{4,5},{5,4},{6,7},{7,6},{8,10},{9,11},{10,... | collective-permute-start | bytes 1572872 | tf_op jit(solution)/shard_map/ppermute | solution.py:66
  17.6 9.7 %collective-permute-done = f32[8,128]{1,0:T(8,128)S(1)} collective-permute-done((f32[8,128]{1,0:T(8,128)S(1)}, f32[8,128]{1,0:T(8,128)S(1)}, u32[]{:S(2)}, u32[]{:S(2)}) %collective-permute-start) | collective-permute-done | bytes 4128 | tf_op jit(solution)/shard_map/ppermute | solution.py:66
  27.3 0.9 collective-permute-start.1
  28.3 2.7 %collective-permute-done.1 = f32[8,128]{1,0:T(8,128)S(1)} collective-permute-done((f32[8,128]{1,0:T(8,128)S(1)}, f32[8,128]{1,0:T(8,128)S(1)}, u32[]{:S(2)}, u32[]{:S(2)}) %collective-permute-start.1) | collective-permute-done | bytes 4128 | tf_op jit(solution)/shard_map/ppermute | solution.py:66
  31.0 3.6 %collective-permute-start.13 = (f32[128,1024]{1,0:T(8,128)}, f32[128,1024]{1,0:T(8,128)S(1)}, u32[]{:S(2)}, u32[]{:S(2)}) collective-permute-start(f32[128,1024]{1,0:T(8,128)} %refs_4_.1), channel_id=1, source_target_pairs={{0,16},{1,17},{2,18},{3,19},{4,12},{5,13},{6,14},{7,15},{8,24},{9,... | collective-permute-start | bytes 1572872 | tf_op jit(solution)/shard_map/ppermute | solution.py:66
  34.6 0.0 collective-permute-done.3.refs_2_
  34.6 0.2 collective-permute-start.19
  34.8 0.1 collective-permute-start.14
  34.9 0.0 collective-permute-done.4.refs_3_
  34.9 1.5 %collective-permute-start.16 = (f32[128,1024]{1,0:T(8,128)S(1)}, f32[128,1024]{1,0:T(8,128)S(1)}, u32[]{:S(2)}, u32[]{:S(2)}) collective-permute-start(f32[128,1024]{1,0:T(8,128)S(1)} %collective-permute-done.12.refs_5_), channel_id=1, source_target_pairs={{0,1},{1,0},{2,3},{3,2},{4,6},{5,7},{6,4},{7,5},{8,9},{9,8},{10,11... | collective-permute-start | bytes 1572872 | tf_op jit(solution)/shard_map/ppermute | solution.py:66
  36.4 1.2 copy-done
  37.6 1.0 copy-done.2
  38.7 1.4 %project.1 = (f32[776,128]{1,0:T(8,128)S(1)}, f32[776,128]{1,0:T(8,128)S(1)}) custom-call(f32[1024,256]{1,0:T(8,128)S(1)} %copy-done, f32[8,128]{1,0:T(8,128)S(1)} %fusion.sums_ref, f32[2,256,256]{2,1,0:T(8,128)S(1)} %copy-done.2, f32[2,256,256]{2,1,0:T(8,128)S(1)} %collective-permute-done.2.refs_1_, f32[2,256,256]{2,1,0:T(8,128)S(1)} %collective-permute-done.3.refs_2_, ...), custom_call_target="tpu_custom_call" | custom-call | flops 2415919104 | bytes 3940352 | tf_op jit(solution)/shard_map/project/pallas_call | solution.py:110
  40.1 0.0 copy-start.4
  40.1 6.3 %collective-permute-done.13.refs_6_ = f32[128,1024]{1,0:T(8,128)S(1)} collective-permute-done((f32[128,1024]{1,0:T(8,128)}, f32[128,1024]{1,0:T(8,128)S(1)}, u32[]{:S(2)}, u32[]{:S(2)}) %collective-permute-start.13) | collective-permute-done | bytes 524320 | tf_op jit(solution)/shard_map/ppermute | solution.py:66
  46.4 2.3 %collective-permute-done.19.refs_12_ = f32[128,1024]{1,0:T(8,128)S(1)} collective-permute-done((f32[128,1024]{1,0:T(8,128)}, f32[128,1024]{1,0:T(8,128)S(1)}, u32[]{:S(2)}, u32[]{:S(2)}) %collective-permute-start.19) | collective-permute-done | bytes 524320 | tf_op jit(solution)/shard_map/ppermute | solution.py:66
  48.7 0.0 collective-permute-start.20
  48.7 0.0 collective-permute-done.23.refs_16_
  48.7 1.1 collective-permute-start.17
  49.8 11.0 %collective-permute-done.14.refs_7_ = f32[128,1024]{1,0:T(8,128)S(1)} collective-permute-done((f32[128,1024]{1,0:T(8,128)S(1)}, f32[128,1024]{1,0:T(8,128)S(1)}, u32[]{:S(2)}, u32[]{:S(2)}) %collective-permute-start.14) | collective-permute-done | bytes 524320 | tf_op jit(solution)/shard_map/ppermute | solution.py:66
  60.8 0.0 collective-permute-start.24
  60.8 0.0 collective-permute-done.16.refs_9_
  60.8 0.4 collective-permute-start.21
  61.2 0.7 collective-permute-start.31
  61.9 0.0 collective-permute-done.20.refs_13_
  62.0 2.7 %collective-permute-start.6 = (f32[776,128]{1,0:T(8,128)S(1)}, f32[776,128]{1,0:T(8,128)S(1)}, u32[]{:S(2)}, u32[]{:S(2)}) collective-permute-start(f32[776,128]{1,0:T(8,128)S(1)} %add.17), channel_id=1, source_target_pairs={{0,8},{1,9},{2,10},{3,11},{4,20},{5,21},{6,22},{7,23},{8,0},{9,1},... | collective-permute-start | bytes 1191944 | tf_op jit(solution)/shard_map/ppermute | solution.py:66
  64.6 13.1 %collective-permute-done.17.refs_10_ = f32[128,1024]{1,0:T(8,128)S(1)} collective-permute-done((f32[128,1024]{1,0:T(8,128)S(1)}, f32[128,1024]{1,0:T(8,128)S(1)}, u32[]{:S(2)}, u32[]{:S(2)}) %collective-permute-start.17) | collective-permute-done | bytes 524320 | tf_op jit(solution)/shard_map/ppermute | solution.py:66
  77.7 0.0 collective-permute-start.25
  77.7 0.5 collective-permute-start.27
  78.2 1.5 %collective-permute-start.18 = (f32[128,1024]{1,0:T(8,128)S(1)}, f32[128,1024]{1,0:T(8,128)S(1)}, u32[]{:S(2)}, u32[]{:S(2)}) collective-permute-start(f32[128,1024]{1,0:T(8,128)S(1)} %collective-permute-done.14.refs_7_), channel_id=1, source_target_pairs={{0,1},{1,0},{2,3},{3,2},{4,6},{5,7},{6,4},{7,5},{8,9},{9,8},{10,11... | collective-permute-start | bytes 1572872 | tf_op jit(solution)/shard_map/ppermute | solution.py:66
  79.7 2.0 %collective-permute-start.22 = (f32[128,1024]{1,0:T(8,128)S(1)}, f32[128,1024]{1,0:T(8,128)S(1)}, u32[]{:S(2)}, u32[]{:S(2)}) collective-permute-start(f32[128,1024]{1,0:T(8,128)S(1)} %collective-permute-done.14.refs_7_), channel_id=1, source_target_pairs={{0,2},{1,3},{2,0},{3,1},{4,5},{5,4},{6,7},{7,6},{8,10},{9,11},{10,... | collective-permute-start | bytes 1572872 | tf_op jit(solution)/shard_map/ppermute | solution.py:66
  81.7 2.0 %collective-permute-start.7 = (f32[776,128]{1,0:T(8,128)S(1)}, f32[776,128]{1,0:T(8,128)S(1)}, u32[]{:S(2)}, u32[]{:S(2)}) collective-permute-start(f32[776,128]{1,0:T(8,128)S(1)} %add.18), channel_id=1, source_target_pairs={{0,16},{1,17},{2,18},{3,19},{4,12},{5,13},{6,14},{7,15},{8,24},{9,... | collective-permute-start | bytes 1191944 | tf_op jit(solution)/shard_map/ppermute | solution.py:66
  83.7 9.0 %collective-permute-done.35.refs_1_ = f32[128,1024]{1,0:T(8,128)S(1)} collective-permute-done((f32[128,1024]{1,0:T(8,128)S(1)}, f32[128,1024]{1,0:T(8,128)S(1)}, u32[]{:S(2)}, u32[]{:S(2)}) %collective-permute-start.35) | collective-permute-done | bytes 524320 | tf_op jit(solution)/shard_map/ppermute | solution.py:66
  92.7 0.3 collective-permute-done.18.refs_11_
  93.1 0.3 collective-permute-start.28
  93.4 5.2 %collective-permute-done.22.refs_15_ = f32[128,1024]{1,0:T(8,128)S(1)} collective-permute-done((f32[128,1024]{1,0:T(8,128)S(1)}, f32[128,1024]{1,0:T(8,128)S(1)}, u32[]{:S(2)}, u32[]{:S(2)}) %collective-permute-start.22) | collective-permute-done | bytes 524320 | tf_op jit(solution)/shard_map/ppermute | solution.py:66
  98.6 0.5 collective-permute-start.29
  99.2 0.1 collective-permute-start.8
  99.3 0.1 collective-permute-start.36
  99.4 0.1 collective-permute-start.37
  99.4 1.1 collective-permute-done.33.refs_26_
  100.5 1.5 %collective-permute-start.34 = (f32[128,1024]{1,0:T(8,128)S(1)}, f32[128,1024]{1,0:T(8,128)S(1)}, u32[]{:S(2)}, u32[]{:S(2)}) collective-permute-start(f32[128,1024]{1,0:T(8,128)S(1)} %collective-permute-done.18.refs_11_), channel_id=1, source_target_pairs={{0,4},{1,5},{2,6},{3,7},{4,0},{5,1},{6,2},{7,3},{8,12},{9,13},{10,... | collective-permute-start | bytes 1572872 | tf_op jit(solution)/shard_map/ppermute | solution.py:66
  102.1 0.1 collective-permute-start.30
  102.1 0.3 collective-permute-start.38
  102.4 1.9 %update.1 = (f32[264,256]{1,0:T(8,128)S(1)}, f32[264,256]{1,0:T(8,128)S(1)}, f32[264,256]{1,0:T(8,128)S(1)}, f32[264,256]{1,0:T(8,128)S(1)}) custom-call(f32[1024,256]{1,0:T(8,128)S(1)} %copy-done, f32[2,256,256]{2,1,0:T(8,128)S(1)} %copy-done.1, f32[776,128]{1,0:T(8,128)S(1)} %add.19.mine_ref, f32[776,128]{1,0:T(8,128)S(1)} %collective-permute-done.8.theirs_ref, ...), custom_call_target="tpu_custom_call" | custom-call | flops 805306368 | bytes 4988928 | tf_op jit(solution)/shard_map/update/pallas_call | solution.py:155
  104.4 4.1 %collective-permute-done.36.refs_2_ = f32[128,1024]{1,0:T(8,128)S(1)} collective-permute-done((f32[128,1024]{1,0:T(8,128)S(1)}, f32[128,1024]{1,0:T(8,128)S(1)}, u32[]{:S(2)}, u32[]{:S(2)}) %collective-permute-start.36) | collective-permute-done | bytes 524320 | tf_op jit(solution)/shard_map/ppermute | solution.py:66
  108.5 0.0 collective-permute-start.10
  108.5 4.8 %collective-permute-done.37.refs_3_ = f32[128,1024]{1,0:T(8,128)S(1)} collective-permute-done((f32[128,1024]{1,0:T(8,128)S(1)}, f32[128,1024]{1,0:T(8,128)S(1)}, u32[]{:S(2)}, u32[]{:S(2)}) %collective-permute-start.37) | collective-permute-done | bytes 524320 | tf_op jit(solution)/shard_map/ppermute | solution.py:66
  113.3 2.2 %collective-permute-start.11 = (f32[264,256]{1,0:T(8,128)S(1)}, f32[264,256]{1,0:T(8,128)S(1)}, u32[]{:S(2)}, u32[]{:S(2)}) collective-permute-start(f32[264,256]{1,0:T(8,128)S(1)} %get-tuple-element.16), channel_id=1, source_target_pairs={{0,3},{1,2},{2,1},{3,0},{4,7},{5,6},{6,5},{7,4},{8,11},{9,10},{10,... | collective-permute-start | bytes 811016 | tf_op jit(solution)/shard_map/ppermute | solution.py:66
  115.5 1.2 collective-permute-start.9
  116.7 0.5 collective-permute-start.40
  117.2 0.1 collective-permute-start.41
  117.3 6.2 %collective-permute-done.11.refs_3_ = f32[264,256]{1,0:T(8,128)S(1)} collective-permute-done((f32[264,256]{1,0:T(8,128)S(1)}, f32[264,256]{1,0:T(8,128)S(1)}, u32[]{:S(2)}, u32[]{:S(2)}) %collective-permute-start.11) | collective-permute-done | bytes 270368 | tf_op jit(solution)/shard_map/ppermute | solution.py:66
  123.4 0.3 collective-permute-start.42
  123.7 1.6 %collective-permute-done.9.refs_1_ = f32[264,256]{1,0:T(8,128)S(1)} collective-permute-done((f32[264,256]{1,0:T(8,128)S(1)}, f32[264,256]{1,0:T(8,128)S(1)}, u32[]{:S(2)}, u32[]{:S(2)}) %collective-permute-start.9) | collective-permute-done | bytes 270368 | tf_op jit(solution)/shard_map/ppermute | solution.py:66
  125.3 8.2 %shard_map.59 = (f32[256,4096]{1,0:T(8,128)}, bf16[512,1024]{1,0:T(8,128)(2,1)S(1)}, f32[2,256]{1,0:T(2,128)}) custom-call(f32[264,256]{1,0:T(8,128)S(1)} %get-tuple-element.13.refs_0_, f32[264,256]{1,0:T(8,128)S(1)} %collective-permute-done.9.refs_1_, f32[264,256]{1,0:T(8,128)S(1)} %collective-permute-done.10.refs_2_, ...), custom_call_target="tpu_custom_call" | custom-call | flops 4831838208 | bytes 15728640 | tf_op jit(solution)/shard_map/pallas_call | solution.py:243
  133.5 3.3 %shard_map.60 = f32[256,4096]{1,0:T(8,128)} custom-call(bf16[512,1024]{1,0:T(8,128)(2,1)S(1)} %get-tuple-element.17.refs_0_, f32[128,1024]{1,0:T(8,128)S(1)} %collective-permute-done.35.refs_1_, f32[128,1024]{1,0:T(8,128)S(1)} %collective-permute-done.36.refs_2_, f32[128,1024]{1,0:T(8,128)S(1)} %collective-permute-done.37.refs_3_, ...), custom_call_target="tpu_custom_call", output_to_operand_aliasing={{}: (9, {})} | custom-call | flops 1610612736 | bytes 5242880 | tf_op jit(solution)/shard_map/pallas_call | solution.py:243
  (43 shorter events, 0.2 us)
Async XLA Ops:
  0.6 15.6 %collective-permute-start.2 = (f32[2,256,256]{2,1,0:T(8,128)}, f32[2,256,256]{2,1,0:T(8,128)S(1)}, u32[]{:S(2)}, u32[]{:S(2)}) collective-permute-start(f32[2,256,256]{2,1,0:T(8,128)} %refs_0_.3), channel_id=1, source_target_pairs={{0,1},{1,0},{2,3},{3,2},{4,6},{5,7},{6,4},{7,5},{8,9},{9,8},{10,11... | collective-permute-start | bytes 1572872 | tf_op jit(solution)/shard_map/ppermute | solution.py:66
  3.7 30.9 %collective-permute-start.3 = (f32[2,256,256]{2,1,0:T(8,128)}, f32[2,256,256]{2,1,0:T(8,128)S(1)}, u32[]{:S(2)}, u32[]{:S(2)}) collective-permute-start(f32[2,256,256]{2,1,0:T(8,128)} %refs_0_.3), channel_id=1, source_target_pairs={{0,2},{1,3},{2,0},{3,1},{4,5},{5,4},{6,7},{7,6},{8,10},{9,11},{10,... | collective-permute-start | bytes 1572872 | tf_op jit(solution)/shard_map/ppermute | solution.py:66
  5.2 29.6 %collective-permute-start.12 = (f32[128,1024]{1,0:T(8,128)}, f32[128,1024]{1,0:T(8,128)S(1)}, u32[]{:S(2)}, u32[]{:S(2)}) collective-permute-start(f32[128,1024]{1,0:T(8,128)} %refs_4_.1), channel_id=1, source_target_pairs={{0,8},{1,9},{2,10},{3,11},{4,20},{5,21},{6,22},{7,23},{8,0},{9,1},... | collective-permute-start | bytes 1572872 | tf_op jit(solution)/shard_map/ppermute | solution.py:66
  6.8 28.0 %collective-permute-start.15 = (f32[128,1024]{1,0:T(8,128)}, f32[128,1024]{1,0:T(8,128)S(1)}, u32[]{:S(2)}, u32[]{:S(2)}) collective-permute-start(f32[128,1024]{1,0:T(8,128)} %refs_4_.1), channel_id=1, source_target_pairs={{0,1},{1,0},{2,3},{3,2},{4,6},{5,7},{6,4},{7,5},{8,9},{9,8},{10,11... | collective-permute-start | bytes 1572872 | tf_op jit(solution)/shard_map/ppermute | solution.py:66
  8.5 18.8 %collective-permute-start = (f32[8,128]{1,0:T(8,128)S(1)}, f32[8,128]{1,0:T(8,128)S(1)}, u32[]{:S(2)}, u32[]{:S(2)}) collective-permute-start(f32[8,128]{1,0:T(8,128)S(1)} %broadcast_in_dim.2), channel_id=1, source_target_pairs={{0,1},{1,0},{2,3},{3,2},{4,6},{5,7},{6,4},{7,5},{8,9},{9,8},{10,11... | collective-permute-start | bytes 12296 | tf_op jit(solution)/shard_map/ppermute | solution.py:66
  16.2 18.7 %collective-permute-start.4 = (f32[2,256,256]{2,1,0:T(8,128)S(1)}, f32[2,256,256]{2,1,0:T(8,128)S(1)}, u32[]{:S(2)}, u32[]{:S(2)}) collective-permute-start(f32[2,256,256]{2,1,0:T(8,128)S(1)} %collective-permute-done.2.refs_1_), channel_id=1, source_target_pairs={{0,2},{1,3},{2,0},{3,1},{4,5},{5,4},{6,7},{7,6},{8,10},{9,11},{10,... | collective-permute-start | bytes 1572872 | tf_op jit(solution)/shard_map/ppermute | solution.py:66
  27.3 3.6 %collective-permute-start.1 = (f32[8,128]{1,0:T(8,128)S(1)}, f32[8,128]{1,0:T(8,128)S(1)}, u32[]{:S(2)}, u32[]{:S(2)}) collective-permute-start(f32[8,128]{1,0:T(8,128)S(1)} %broadcast_add_fusion), channel_id=1, source_target_pairs={{0,2},{1,3},{2,0},{3,1},{4,5},{5,4},{6,7},{7,6},{8,10},{9,11},{10,... | collective-permute-start | bytes 12296 | tf_op jit(solution)/shard_map/ppermute | solution.py:66
  31.0 15.5 %collective-permute-start.13 = (f32[128,1024]{1,0:T(8,128)}, f32[128,1024]{1,0:T(8,128)S(1)}, u32[]{:S(2)}, u32[]{:S(2)}) collective-permute-start(f32[128,1024]{1,0:T(8,128)} %refs_4_.1), channel_id=1, source_target_pairs={{0,16},{1,17},{2,18},{3,19},{4,12},{5,13},{6,14},{7,15},{8,24},{9,... | collective-permute-start | bytes 1572872 | tf_op jit(solution)/shard_map/ppermute | solution.py:66
  34.6 14.1 %collective-permute-start.19 = (f32[128,1024]{1,0:T(8,128)}, f32[128,1024]{1,0:T(8,128)S(1)}, u32[]{:S(2)}, u32[]{:S(2)}) collective-permute-start(f32[128,1024]{1,0:T(8,128)} %refs_4_.1), channel_id=1, source_target_pairs={{0,2},{1,3},{2,0},{3,1},{4,5},{5,4},{6,7},{7,6},{8,10},{9,11},{10,... | collective-permute-start | bytes 1572872 | tf_op jit(solution)/shard_map/ppermute | solution.py:66
  34.8 13.9 %collective-permute-start.23 = (f32[128,1024]{1,0:T(8,128)}, f32[128,1024]{1,0:T(8,128)S(1)}, u32[]{:S(2)}, u32[]{:S(2)}) collective-permute-start(f32[128,1024]{1,0:T(8,128)} %refs_4_.1), channel_id=1, source_target_pairs={{0,4},{1,5},{2,6},{3,7},{4,0},{5,1},{6,2},{7,3},{8,12},{9,13},{10,... | collective-permute-start | bytes 1572872 | tf_op jit(solution)/shard_map/ppermute | solution.py:66
  34.8 26.0 %collective-permute-start.14 = (f32[128,1024]{1,0:T(8,128)S(1)}, f32[128,1024]{1,0:T(8,128)S(1)}, u32[]{:S(2)}, u32[]{:S(2)}) collective-permute-start(f32[128,1024]{1,0:T(8,128)S(1)} %collective-permute-done.12.refs_5_), channel_id=1, source_target_pairs={{0,16},{1,17},{2,18},{3,19},{4,12},{5,13},{6,14},{7,15},{8,24},{9,... | collective-permute-start | bytes 1572872 | tf_op jit(solution)/shard_map/ppermute | solution.py:66
  34.9 25.9 %collective-permute-start.16 = (f32[128,1024]{1,0:T(8,128)S(1)}, f32[128,1024]{1,0:T(8,128)S(1)}, u32[]{:S(2)}, u32[]{:S(2)}) collective-permute-start(f32[128,1024]{1,0:T(8,128)S(1)} %collective-permute-done.12.refs_5_), channel_id=1, source_target_pairs={{0,1},{1,0},{2,3},{3,2},{4,6},{5,7},{6,4},{7,5},{8,9},{9,8},{10,11... | collective-permute-start | bytes 1572872 | tf_op jit(solution)/shard_map/ppermute | solution.py:66
  36.4 1.2 copy-start
  37.6 1.0 copy-start.2
  38.7 63.7 %copy-start.1 = (f32[2,256,256]{2,1,0:T(8,128)S(1)}, f32[2,256,256]{2,1,0:T(8,128)}, u32[]{:S(2)}) copy-start(f32[2,256,256]{2,1,0:T(8,128)} %factors_ref.1) | copy-start | bytes 1572868
  38.7 63.7 %copy-start.3 = (f32[2,256,256]{2,1,0:T(8,128)S(1)}, f32[2,256,256]{2,1,0:T(8,128)}, u32[]{:S(2)}) copy-start(f32[2,256,256]{2,1,0:T(8,128)} %refs_0_.3) | copy-start | bytes 1572868
  40.1 85.2 %copy-start.4 = (f32[128,1024]{1,0:T(8,128)S(1)}, f32[128,1024]{1,0:T(8,128)}, u32[]{:S(2)}) copy-start(f32[128,1024]{1,0:T(8,128)} %refs_4_.1) | copy-start | bytes 1572868
  46.4 14.8 %collective-permute-start.5 = (f32[776,128]{1,0:T(8,128)S(1)}, f32[776,128]{1,0:T(8,128)S(1)}, u32[]{:S(2)}, u32[]{:S(2)}) collective-permute-start(f32[776,128]{1,0:T(8,128)S(1)} %get-tuple-element.12), channel_id=1, source_target_pairs={{0,4},{1,5},{2,6},{3,7},{4,0},{5,1},{6,2},{7,3},{8,12},{9,13},{10,... | collective-permute-start | bytes 1191944 | tf_op jit(solution)/shard_map/ppermute | solution.py:66
  48.7 13.3 %collective-permute-start.20 = (f32[128,1024]{1,0:T(8,128)S(1)}, f32[128,1024]{1,0:T(8,128)S(1)}, u32[]{:S(2)}, u32[]{:S(2)}) collective-permute-start(f32[128,1024]{1,0:T(8,128)S(1)} %collective-permute-done.12.refs_5_), channel_id=1, source_target_pairs={{0,2},{1,3},{2,0},{3,1},{4,5},{5,4},{6,7},{7,6},{8,10},{9,11},{10,... | collective-permute-start | bytes 1572872 | tf_op jit(solution)/shard_map/ppermute | solution.py:66
  48.7 29.0 %collective-permute-start.17 = (f32[128,1024]{1,0:T(8,128)S(1)}, f32[128,1024]{1,0:T(8,128)S(1)}, u32[]{:S(2)}, u32[]{:S(2)}) collective-permute-start(f32[128,1024]{1,0:T(8,128)S(1)} %collective-permute-done.15.refs_8_), channel_id=1, source_target_pairs={{0,16},{1,17},{2,18},{3,19},{4,12},{5,13},{6,14},{7,15},{8,24},{9,... | collective-permute-start | bytes 1572872 | tf_op jit(solution)/shard_map/ppermute | solution.py:66
  60.8 16.9 %collective-permute-start.24 = (f32[128,1024]{1,0:T(8,128)S(1)}, f32[128,1024]{1,0:T(8,128)S(1)}, u32[]{:S(2)}, u32[]{:S(2)}) collective-permute-start(f32[128,1024]{1,0:T(8,128)S(1)} %collective-permute-done.12.refs_5_), channel_id=1, source_target_pairs={{0,4},{1,5},{2,6},{3,7},{4,0},{5,1},{6,2},{7,3},{8,12},{9,13},{10,... | collective-permute-start | bytes 1572872 | tf_op jit(solution)/shard_map/ppermute | solution.py:66
  60.8 17.4 %collective-permute-start.21 = (f32[128,1024]{1,0:T(8,128)S(1)}, f32[128,1024]{1,0:T(8,128)S(1)}, u32[]{:S(2)}, u32[]{:S(2)}) collective-permute-start(f32[128,1024]{1,0:T(8,128)S(1)} %collective-permute-done.13.refs_6_), channel_id=1, source_target_pairs={{0,2},{1,3},{2,0},{3,1},{4,5},{5,4},{6,7},{7,6},{8,10},{9,11},{10,... | collective-permute-start | bytes 1572872 | tf_op jit(solution)/shard_map/ppermute | solution.py:66
  61.2 17.0 %collective-permute-start.31 = (f32[128,1024]{1,0:T(8,128)S(1)}, f32[128,1024]{1,0:T(8,128)S(1)}, u32[]{:S(2)}, u32[]{:S(2)}) collective-permute-start(f32[128,1024]{1,0:T(8,128)S(1)} %collective-permute-done.15.refs_8_), channel_id=1, source_target_pairs={{0,4},{1,5},{2,6},{3,7},{4,0},{5,1},{6,2},{7,3},{8,12},{9,13},{10,... | collective-permute-start | bytes 1572872 | tf_op jit(solution)/shard_map/ppermute | solution.py:66
  62.0 17.8 %collective-permute-start.6 = (f32[776,128]{1,0:T(8,128)S(1)}, f32[776,128]{1,0:T(8,128)S(1)}, u32[]{:S(2)}, u32[]{:S(2)}) collective-permute-start(f32[776,128]{1,0:T(8,128)S(1)} %add.17), channel_id=1, source_target_pairs={{0,8},{1,9},{2,10},{3,11},{4,20},{5,21},{6,22},{7,23},{8,0},{9,1},... | collective-permute-start | bytes 1191944 | tf_op jit(solution)/shard_map/ppermute | solution.py:66
  77.7 4.0 %collective-permute-start.25 = (f32[128,1024]{1,0:T(8,128)S(1)}, f32[128,1024]{1,0:T(8,128)S(1)}, u32[]{:S(2)}, u32[]{:S(2)}) collective-permute-start(f32[128,1024]{1,0:T(8,128)S(1)} %collective-permute-done.13.refs_6_), channel_id=1, source_target_pairs={{0,4},{1,5},{2,6},{3,7},{4,0},{5,1},{6,2},{7,3},{8,12},{9,13},{10,... | collective-permute-start | bytes 1572872 | tf_op jit(solution)/shard_map/ppermute | solution.py:66
  77.7 6.1 %collective-permute-start.27 = (f32[128,1024]{1,0:T(8,128)S(1)}, f32[128,1024]{1,0:T(8,128)S(1)}, u32[]{:S(2)}, u32[]{:S(2)}) collective-permute-start(f32[128,1024]{1,0:T(8,128)S(1)} %collective-permute-done.19.refs_12_), channel_id=1, source_target_pairs={{0,4},{1,5},{2,6},{3,7},{4,0},{5,1},{6,2},{7,3},{8,12},{9,13},{10,... | collective-permute-start | bytes 1572872 | tf_op jit(solution)/shard_map/ppermute | solution.py:66
  78.2 14.5 %collective-permute-start.35 = (f32[128,1024]{1,0:T(8,128)S(1)}, f32[128,1024]{1,0:T(8,128)S(1)}, u32[]{:S(2)}, u32[]{:S(2)}) collective-permute-start(f32[128,1024]{1,0:T(8,128)S(1)} %collective-permute-done.15.refs_8_), channel_id=1, source_target_pairs={{0,2},{1,3},{2,0},{3,1},{4,5},{5,4},{6,7},{7,6},{8,10},{9,11},{10,... | collective-permute-start | bytes 1572872 | tf_op jit(solution)/shard_map/ppermute | solution.py:66
  78.2 14.9 %collective-permute-start.18 = (f32[128,1024]{1,0:T(8,128)S(1)}, f32[128,1024]{1,0:T(8,128)S(1)}, u32[]{:S(2)}, u32[]{:S(2)}) collective-permute-start(f32[128,1024]{1,0:T(8,128)S(1)} %collective-permute-done.14.refs_7_), channel_id=1, source_target_pairs={{0,1},{1,0},{2,3},{3,2},{4,6},{5,7},{6,4},{7,5},{8,9},{9,8},{10,11... | collective-permute-start | bytes 1572872 | tf_op jit(solution)/shard_map/ppermute | solution.py:66
  79.7 18.9 %collective-permute-start.22 = (f32[128,1024]{1,0:T(8,128)S(1)}, f32[128,1024]{1,0:T(8,128)S(1)}, u32[]{:S(2)}, u32[]{:S(2)}) collective-permute-start(f32[128,1024]{1,0:T(8,128)S(1)} %collective-permute-done.14.refs_7_), channel_id=1, source_target_pairs={{0,2},{1,3},{2,0},{3,1},{4,5},{5,4},{6,7},{7,6},{8,10},{9,11},{10,... | collective-permute-start | bytes 1572872 | tf_op jit(solution)/shard_map/ppermute | solution.py:66
  81.7 16.9 %collective-permute-start.7 = (f32[776,128]{1,0:T(8,128)S(1)}, f32[776,128]{1,0:T(8,128)S(1)}, u32[]{:S(2)}, u32[]{:S(2)}) collective-permute-start(f32[776,128]{1,0:T(8,128)S(1)} %add.18), channel_id=1, source_target_pairs={{0,16},{1,17},{2,18},{3,19},{4,12},{5,13},{6,14},{7,15},{8,24},{9,... | collective-permute-start | bytes 1191944 | tf_op jit(solution)/shard_map/ppermute | solution.py:66
  83.7 15.4 %collective-permute-start.26 = (f32[128,1024]{1,0:T(8,128)S(1)}, f32[128,1024]{1,0:T(8,128)S(1)}, u32[]{:S(2)}, u32[]{:S(2)}) collective-permute-start(f32[128,1024]{1,0:T(8,128)S(1)} %collective-permute-done.14.refs_7_), channel_id=1, source_target_pairs={{0,4},{1,5},{2,6},{3,7},{4,0},{5,1},{6,2},{7,3},{8,12},{9,13},{10,... | collective-permute-start | bytes 1572872 | tf_op jit(solution)/shard_map/ppermute | solution.py:66
  92.7 6.5 %collective-permute-start.32 = (f32[128,1024]{1,0:T(8,128)S(1)}, f32[128,1024]{1,0:T(8,128)S(1)}, u32[]{:S(2)}, u32[]{:S(2)}) collective-permute-start(f32[128,1024]{1,0:T(8,128)S(1)} %collective-permute-done.16.refs_9_), channel_id=1, source_target_pairs={{0,4},{1,5},{2,6},{3,7},{4,0},{5,1},{6,2},{7,3},{8,12},{9,13},{10,... | collective-permute-start | bytes 1572872 | tf_op jit(solution)/shard_map/ppermute | solution.py:66
  93.1 6.3 %collective-permute-start.28 = (f32[128,1024]{1,0:T(8,128)S(1)}, f32[128,1024]{1,0:T(8,128)S(1)}, u32[]{:S(2)}, u32[]{:S(2)}) collective-permute-start(f32[128,1024]{1,0:T(8,128)S(1)} %collective-permute-done.20.refs_13_), channel_id=1, source_target_pairs={{0,4},{1,5},{2,6},{3,7},{4,0},{5,1},{6,2},{7,3},{8,12},{9,13},{10,... | collective-permute-start | bytes 1572872 | tf_op jit(solution)/shard_map/ppermute | solution.py:66
  98.6 1.9 %collective-permute-start.33 = (f32[128,1024]{1,0:T(8,128)S(1)}, f32[128,1024]{1,0:T(8,128)S(1)}, u32[]{:S(2)}, u32[]{:S(2)}) collective-permute-start(f32[128,1024]{1,0:T(8,128)S(1)} %collective-permute-done.17.refs_10_), channel_id=1, source_target_pairs={{0,4},{1,5},{2,6},{3,7},{4,0},{5,1},{6,2},{7,3},{8,12},{9,13},{10,... | collective-permute-start | bytes 1572872 | tf_op jit(solution)/shard_map/ppermute | solution.py:66
  98.6 3.4 %collective-permute-start.29 = (f32[128,1024]{1,0:T(8,128)S(1)}, f32[128,1024]{1,0:T(8,128)S(1)}, u32[]{:S(2)}, u32[]{:S(2)}) collective-permute-start(f32[128,1024]{1,0:T(8,128)S(1)} %collective-permute-done.21.refs_14_), channel_id=1, source_target_pairs={{0,4},{1,5},{2,6},{3,7},{4,0},{5,1},{6,2},{7,3},{8,12},{9,13},{10,... | collective-permute-start | bytes 1572872 | tf_op jit(solution)/shard_map/ppermute | solution.py:66
  99.2 3.0 %collective-permute-start.8 = (f32[776,128]{1,0:T(8,128)S(1)}, f32[776,128]{1,0:T(8,128)S(1)}, u32[]{:S(2)}, u32[]{:S(2)}) collective-permute-start(f32[776,128]{1,0:T(8,128)S(1)} %add.19.mine_ref), channel_id=1, source_target_pairs={{0,4},{1,5},{2,6},{3,7},{4,0},{5,1},{6,2},{7,3},{8,12},{9,13},{10,... | collective-permute-start | bytes 1191944 | tf_op jit(solution)/shard_map/ppermute | solution.py:66
  99.3 9.2 %collective-permute-start.36 = (f32[128,1024]{1,0:T(8,128)S(1)}, f32[128,1024]{1,0:T(8,128)S(1)}, u32[]{:S(2)}, u32[]{:S(2)}) collective-permute-start(f32[128,1024]{1,0:T(8,128)S(1)} %collective-permute-done.16.refs_9_), channel_id=1, source_target_pairs={{0,2},{1,3},{2,0},{3,1},{4,5},{5,4},{6,7},{7,6},{8,10},{9,11},{10,... | collective-permute-start | bytes 1572872 | tf_op jit(solution)/shard_map/ppermute | solution.py:66
  99.4 14.0 %collective-permute-start.37 = (f32[128,1024]{1,0:T(8,128)S(1)}, f32[128,1024]{1,0:T(8,128)S(1)}, u32[]{:S(2)}, u32[]{:S(2)}) collective-permute-start(f32[128,1024]{1,0:T(8,128)S(1)} %collective-permute-done.35.refs_1_), channel_id=1, source_target_pairs={{0,16},{1,17},{2,18},{3,19},{4,12},{5,13},{6,14},{7,15},{8,24},{9,... | collective-permute-start | bytes 1572872 | tf_op jit(solution)/shard_map/ppermute | solution.py:66
  100.5 15.0 %collective-permute-start.34 = (f32[128,1024]{1,0:T(8,128)S(1)}, f32[128,1024]{1,0:T(8,128)S(1)}, u32[]{:S(2)}, u32[]{:S(2)}) collective-permute-start(f32[128,1024]{1,0:T(8,128)S(1)} %collective-permute-done.18.refs_11_), channel_id=1, source_target_pairs={{0,4},{1,5},{2,6},{3,7},{4,0},{5,1},{6,2},{7,3},{8,12},{9,13},{10,... | collective-permute-start | bytes 1572872 | tf_op jit(solution)/shard_map/ppermute | solution.py:66
  102.1 14.6 %collective-permute-start.30 = (f32[128,1024]{1,0:T(8,128)S(1)}, f32[128,1024]{1,0:T(8,128)S(1)}, u32[]{:S(2)}, u32[]{:S(2)}) collective-permute-start(f32[128,1024]{1,0:T(8,128)S(1)} %collective-permute-done.22.refs_15_), channel_id=1, source_target_pairs={{0,4},{1,5},{2,6},{3,7},{4,0},{5,1},{6,2},{7,3},{8,12},{9,13},{10,... | collective-permute-start | bytes 1572872 | tf_op jit(solution)/shard_map/ppermute | solution.py:66
  102.1 14.5 %collective-permute-start.38 = (f32[128,1024]{1,0:T(8,128)S(1)}, f32[128,1024]{1,0:T(8,128)S(1)}, u32[]{:S(2)}, u32[]{:S(2)}) collective-permute-start(f32[128,1024]{1,0:T(8,128)S(1)} %collective-permute-done.18.refs_11_), channel_id=1, source_target_pairs={{0,2},{1,3},{2,0},{3,1},{4,5},{5,4},{6,7},{7,6},{8,10},{9,11},{10,... | collective-permute-start | bytes 1572872 | tf_op jit(solution)/shard_map/ppermute | solution.py:66
  108.5 8.7 %collective-permute-start.10 = (f32[264,256]{1,0:T(8,128)S(1)}, f32[264,256]{1,0:T(8,128)S(1)}, u32[]{:S(2)}, u32[]{:S(2)}) collective-permute-start(f32[264,256]{1,0:T(8,128)S(1)} %get-tuple-element.15), channel_id=1, source_target_pairs={{0,2},{1,3},{2,0},{3,1},{4,5},{5,4},{6,7},{7,6},{8,10},{9,11},{10,... | collective-permute-start | bytes 811016 | tf_op jit(solution)/shard_map/ppermute | solution.py:66
  113.3 10.1 %collective-permute-start.11 = (f32[264,256]{1,0:T(8,128)S(1)}, f32[264,256]{1,0:T(8,128)S(1)}, u32[]{:S(2)}, u32[]{:S(2)}) collective-permute-start(f32[264,256]{1,0:T(8,128)S(1)} %get-tuple-element.16), channel_id=1, source_target_pairs={{0,3},{1,2},{2,1},{3,0},{4,7},{5,6},{6,5},{7,4},{8,11},{9,10},{10,... | collective-permute-start | bytes 811016 | tf_op jit(solution)/shard_map/ppermute | solution.py:66
  115.5 9.8 %collective-permute-start.9 = (f32[264,256]{1,0:T(8,128)S(1)}, f32[264,256]{1,0:T(8,128)S(1)}, u32[]{:S(2)}, u32[]{:S(2)}) collective-permute-start(f32[264,256]{1,0:T(8,128)S(1)} %get-tuple-element.14), channel_id=1, source_target_pairs={{0,1},{1,0},{2,3},{3,2},{4,6},{5,7},{6,4},{7,5},{8,9},{9,8},{10,11... | collective-permute-start | bytes 811016 | tf_op jit(solution)/shard_map/ppermute | solution.py:66
  116.7 16.8 %collective-permute-start.39 = (f32[128,1024]{1,0:T(8,128)S(1)}, f32[128,1024]{1,0:T(8,128)S(1)}, u32[]{:S(2)}, u32[]{:S(2)}) collective-permute-start(f32[128,1024]{1,0:T(8,128)S(1)} %collective-permute-done.35.refs_1_), channel_id=1, source_target_pairs={{0,4},{1,5},{2,6},{3,7},{4,0},{5,1},{6,2},{7,3},{8,12},{9,13},{10,... | collective-permute-start | bytes 1572872 | tf_op jit(solution)/shard_map/ppermute | solution.py:66
  116.7 16.8 %collective-permute-start.40 = (f32[128,1024]{1,0:T(8,128)S(1)}, f32[128,1024]{1,0:T(8,128)S(1)}, u32[]{:S(2)}, u32[]{:S(2)}) collective-permute-start(f32[128,1024]{1,0:T(8,128)S(1)} %collective-permute-done.36.refs_2_), channel_id=1, source_target_pairs={{0,4},{1,5},{2,6},{3,7},{4,0},{5,1},{6,2},{7,3},{8,12},{9,13},{10,... | collective-permute-start | bytes 1572872 | tf_op jit(solution)/shard_map/ppermute | solution.py:66
  117.2 16.3 %collective-permute-start.41 = (f32[128,1024]{1,0:T(8,128)S(1)}, f32[128,1024]{1,0:T(8,128)S(1)}, u32[]{:S(2)}, u32[]{:S(2)}) collective-permute-start(f32[128,1024]{1,0:T(8,128)S(1)} %collective-permute-done.37.refs_3_), channel_id=1, source_target_pairs={{0,4},{1,5},{2,6},{3,7},{4,0},{5,1},{6,2},{7,3},{8,12},{9,13},{10,... | collective-permute-start | bytes 1572872 | tf_op jit(solution)/shard_map/ppermute | solution.py:66
  123.4 10.1 %collective-permute-start.42 = (f32[128,1024]{1,0:T(8,128)S(1)}, f32[128,1024]{1,0:T(8,128)S(1)}, u32[]{:S(2)}, u32[]{:S(2)}) collective-permute-start(f32[128,1024]{1,0:T(8,128)S(1)} %collective-permute-done.38.refs_4_), channel_id=1, source_target_pairs={{0,4},{1,5},{2,6},{3,7},{4,0},{5,1},{6,2},{7,3},{8,12},{9,13},{10,... | collective-permute-start | bytes 1572872 | tf_op jit(solution)/shard_map/ppermute | solution.py:66
